TPU v7x, 768 devices: a whole 4x8x12 slice. The times are simulated.
768 devices in a mesh: grp: 48 (over z_hi, y, core), tp: 16 (over z_lo, x).
Axes of the slice: x: 4, y: 8, z: 12 (z_hi: 3, z_lo: 4; z = z_hi * 4 + z_lo), core: 2. Of those that a mesh axis runs over, the one named last changes fastest.
Arguments:
- text_embeds: bfloat16 [98304, 8192], P('grp', 'tp'), may hold values from -6 to 6
- image_embeds: bfloat16 [49152, 8192], P(('grp', 'tp')), may hold values from -6 to 6
- image_offsets: int32 [96, 2], P('grp'), may hold values from 0 to 768, as said below
- image_counts: int32 [96], P('grp'), may hold values from 1 to 2
- seq_lengths: int32 [96], P('grp'), may hold values from 513 to 1024
- norm_gain: bfloat16 [8192], P('tp'), may hold values from 0.25 to 1.75
- key_weight: bfloat16 [8192, 512], P('tp'), may hold values from -0.0625 to 0.0625
- key_bias: bfloat16 [512], replicated, may hold values from -3 to 3
- key_cotangent: bfloat16 [98304, 512], P(('grp', 'tp')), may hold values from -0.017944336 to 0.017944336
Outputs:
- key_states: bfloat16 [98304, 512], P(('grp', 'tp'))
- weight_grad: float32 [8192, 512], P('tp')
- bias_grad: float32 [512], replicated
- gain_grad: float32 [8192], P('tp')
Inputs may be any that keep to these rules, and one draw needn't show every extreme that they name: `image_offsets`: each sequence's first image_counts slots hold increasing starts of non-intersecting runs of 256 rows that end within its used rows; later slots hold 0.
All inputs are finite; a program needn't handle non-finite values.
Results may differ from a plain program's by a relative error of at most 0.0046.
Values may be sent and summed in bfloat16 or wider, within the bound.
No kernel may reach another device: no remote copies, remote signals or barrier semaphores. Data moves between devices by JAX's collectives and lax.ppermute only.
A program may use at most 32 MiB of HBM per device.

v0:
```python
import jax
import jax.numpy as jnp
from jax import lax
from jax.sharding import PartitionSpec as P

D = 8192
PATCH_TOK = 256
MAX_IMG = 2
LEN = 1024


def copy_for_each(value, axis):
    devices = lax.axis_size(axis)
    return lax.all_to_all(
        jnp.broadcast_to(value[None], (devices, *value.shape)), axis, 0, 0, tiled=True
    )


def over_copies(value, axis):
    return copy_for_each(value, axis).sum(axis=0)


def in_order(pieces, dim):
    shape = list(pieces.shape[1:])
    shape[dim] *= pieces.shape[0]
    return jnp.moveaxis(pieces, 0, dim).reshape(shape)


def gathered_copies(value, axis, dim):
    return in_order(copy_for_each(value, axis), dim)


def place_images(text_rows, image_rows, offsets, counts, lengths):
    total_rows = text_rows.shape[0]
    row_ids = jnp.arange(total_rows, dtype=jnp.int32)
    seq_ids = row_ids // LEN
    position = row_ids % LEN
    seq_hot = (seq_ids[:, None] == jnp.arange(offsets.shape[0], dtype=jnp.int32)[None, :]).astype(
        jnp.int32
    )
    row_offsets = jnp.sum(seq_hot[:, :, None] * offsets[None, :, :], axis=1)
    row_counts = jnp.sum(seq_hot * counts[None, :], axis=1)
    row_lengths = jnp.sum(seq_hot * lengths[None, :], axis=1)
    slot_ids = jnp.arange(MAX_IMG, dtype=jnp.int32)
    inside = (
        (slot_ids[None, :] < row_counts[:, None])
        & (position[:, None] >= row_offsets)
        & (position[:, None] < row_offsets + PATCH_TOK)
    )
    inside_int = inside.astype(jnp.int32)
    any_inside = jnp.sum(inside_int, axis=1) > 0
    chosen_slot = jnp.sum(inside_int * slot_ids[None, :], axis=1)
    chosen_start = jnp.sum(inside_int * row_offsets, axis=1)
    source = (seq_ids * MAX_IMG + chosen_slot) * PATCH_TOK + position - chosen_start
    source = jnp.where(any_inside, source, 0)
    picked = jnp.take(image_rows, source, axis=0)
    merged = jnp.where(any_inside[:, None], picked, text_rows)
    row_valid = (position < row_lengths).astype(jnp.float32)
    return (merged, row_valid)


def on_device(
    text_embeds,
    image_embeds,
    image_offsets,
    image_counts,
    seq_lengths,
    norm_gain,
    key_weight,
    key_bias,
    key_cotangent,
):
    image_rows = lax.all_to_all(image_embeds, "tp", split_axis=1, concat_axis=0, tiled=True)
    merged, row_valid = place_images(
        text_embeds, image_rows, image_offsets, image_counts, seq_lengths
    )
    merged32 = merged.astype(jnp.float32)
    squares = over_copies(jnp.sum(merged32 * merged32, axis=1), "tp")
    rstd = lax.rsqrt(squares / D + 1e-06)
    gain32 = norm_gain.astype(jnp.float32)
    normed = (merged32 * rstd[:, None] * gain32[None, :]).astype(jnp.bfloat16)
    own_count = key_cotangent.shape[0]
    projected = lax.psum_scatter(
        jnp.dot(normed, key_weight, preferred_element_type=jnp.float32),
        "tp",
        scatter_dimension=0,
        tiled=True,
    )
    own_valid = lax.dynamic_slice_in_dim(row_valid, lax.axis_index("tp") * own_count, own_count, 0)
    bias32 = key_bias.astype(jnp.float32)
    key_states = ((projected + bias32[None, :]) * own_valid[:, None]).astype(jnp.bfloat16)
    own_grad = (key_cotangent.astype(jnp.float32) * own_valid[:, None]).astype(jnp.bfloat16)
    masked_grad = gathered_copies(own_grad, "tp", 0)
    weight_local = lax.dot_general(
        normed, masked_grad, (((0,), (0,)), ((), ())), preferred_element_type=jnp.float32
    )
    bias_local = jnp.sum(masked_grad.astype(jnp.float32), axis=0)
    grad_normed = lax.dot_general(
        masked_grad, key_weight, (((1,), (1,)), ((), ())), preferred_element_type=jnp.float32
    )
    gain_local = jnp.sum(grad_normed * merged32 * rstd[:, None], axis=0)
    weight_grad, bias_grad, gain_grad = lax.psum((weight_local, bias_local, gain_local), "grp")
    return (key_states, weight_grad, bias_grad, gain_grad)


def solution(mesh):
    placed = (
        P("grp", "tp"),
        P(("grp", "tp"), None),
        P("grp", None),
        P("grp"),
        P("grp"),
        P("tp"),
        P("tp", None),
        P(),
        P(("grp", "tp"), None),
    )
    return jax.shard_map(
        on_device,
        mesh=mesh,
        in_specs=placed,
        out_specs=(P(("grp", "tp"), None), P("tp", None), P(), P("tp")),
        check_vma=False,
    )
```

profile of v0, /device:TPU:1, one launch (start us, length us, event | category | flops | bytes accessed | tf_op | source)
XLA Modules:
  0.0 737.8 jit_solution(12849253708947124913)
XLA Ops:
  7.2 0.0 copy-start
  7.2 0.0 copy-start.5
  7.2 0.0 copy-start.8
  7.2 0.0 copy-start.9
  7.2 2.4 copy.21
  9.6 10.4 %all-to-all-start = ((bf16[64,16,512]{2,0,1:T(8,128)(2,1)}), bf16[64,16,512]{2,0,1:T(8,128)(2,1)S(1)}, u32[]{:S(2)}, u32[]{:S(2)}) async-start(bf16[64,16,512]{2,0,1:T(8,128)(2,1)} %bitcast.14), calls=%async_computation | async-start | bytes 2097152 | tf_op jit(solution)/shard_map/all_to_all | solution.py:73
  20.0 0.0 copy-done.5
  20.0 0.1 multiply_reduce_fusion
  20.1 0.0 copy-done.8
  20.1 0.0 copy-done.9
  20.1 0.1 select_reduce_fusion
  20.2 0.1 select_reduce_fusion.2
  20.4 20.9 %all-to-all-done = bf16[64,16,512]{2,0,1:T(8,128)(2,1)S(1)} async-done(((bf16[64,16,512]{2,0,1:T(8,128)(2,1)}), bf16[64,16,512]{2,0,1:T(8,128)(2,1)S(1)}, u32[]{:S(2)}, u32[]{:S(2)}) %all-to-all-start) | async-done | bytes 1048608 | tf_op jit(solution)/shard_map/all_to_all | solution.py:73
  41.3 9.2 %gather_fusion = bf16[2048,512]{1,0:T(8,128)(2,1)} fusion(bf16[1024,512]{1,0:T(8,128)(2,1)S(1)} %bitcast.15, s32[2048]{0:T(1024)S(1)} %broadcast_clamp_fusion), kind=kCustom, calls=%fused_computation | custom fusion | bytes 4202496 | tf_op jit(solution)/shard_map/jit(_take)/gather | solution.py:56
  50.4 0.0 copy-start.6
  50.4 3.1 fusion
  53.5 0.0 copy-start.1
  53.5 0.8 broadcast_in_dim.27
  54.3 8.0 %all-to-all-start.1 = ((f32[16,1,2048]{2,1,0:T(1,128)}), f32[16,1,2048]{2,1,0:T(1,128)S(1)}, u32[]{:S(2)}, u32[]{:S(2)}) async-start(f32[16,1,2048]{2,1,0:T(1,128)} %broadcast_in_dim.27), calls=%async_computation.1 | async-start | bytes 262144 | tf_op jit(solution)/shard_map/all_to_all | solution.py:14
  62.4 0.0 reduce-scatter.2.cloned.1.call-start
  62.4 0.0 copy-done.6
  62.4 7.7 %all-to-all-done.1 = f32[16,1,2048]{2,1,0:T(1,128)S(1)} async-done(((f32[16,1,2048]{2,1,0:T(1,128)}), f32[16,1,2048]{2,1,0:T(1,128)S(1)}, u32[]{:S(2)}, u32[]{:S(2)}) %all-to-all-start.1) | async-done | bytes 131104 | tf_op jit(solution)/shard_map/all_to_all | solution.py:14
  70.2 0.1 reduce_sum.102
  70.3 0.0 copy-done
  70.3 3.2 fusion.7
  73.5 0.0 copy-done.1
  73.5 0.0 copy-start.7
  73.5 0.0 copy-start.4
  73.5 0.0 reduce-scatter.2.cloned.1.call-update
  73.6 0.0 all-reduce.3.cloned.1.call-start
  73.6 0.6 copy-done.7
  74.2 0.1 compare_convert_fusion
  74.3 93.3 %reduce-scatter.2.cloned.1.call-done = f32[128,512]{1,0:T(8,128)} async-done(((f32[2048,512]{1,0:T(8,128)}), f32[128,512]{1,0:T(8,128)}) %reduce-scatter.2.cloned.1.call-update) | async-done | bytes 262160 | tf_op jit(solution)/shard_map/reduce_scatter | solution.py:83
  167.6 0.0 copy-done.4
  167.6 1.7 multiply_convert_fusion
  169.3 0.2 broadcast_in_dim.28
  169.5 0.0 copy-start.2
  169.6 46.6 %all_to_all.30 = bf16[16,128,512]{2,1,0:T(8,128)(2,1)S(1)} all-to-all(bf16[16,128,512]{2,1,0:T(8,128)(2,1)S(1)} %broadcast_in_dim.28), channel_id=1, replica_groups=mesh['grp'=48,'tp'=16] {'tp'}, dimensions={0} | all-to-all | bytes 4194304 | tf_op jit(solution)/shard_map/all_to_all | solution.py:14
  216.1 0.0 copy-done.2
  216.1 2.4 fusion.5
  218.5 0.0 all-reduce.3.cloned.1.call-update
  218.6 0.0 copy-start.3
  218.6 0.3 convert_reduce_fusion
  218.9 1.2 copy-done.3
  220.2 1.4 fusion.4
  221.6 132.3 %all-reduce = (f32[512]{0:T(512)}, f32[512]{0:T(512)}) all-reduce(f32[512]{0:T(512)S(1)} %convert_reduce_fusion, f32[512]{0:T(512)S(1)} %fusion.4), channel_id=1, replica_groups=mesh['grp'=48,'tp'=16] {'grp'}, use_global_device_ids=true, to_apply=%region_11.12 | all-reduce | flops 1024 | bytes 8192 | tf_op jit(solution)/shard_map/psum | solution.py:102
  353.8 374.9 %all-reduce.3.cloned.1.call-done = f32[512,512]{1,0:T(8,128)} async-done(((f32[512,512]{1,0:T(8,128)}), f32[512,512]{1,0:T(8,128)}) %all-reduce.3.cloned.1.call-update) | async-done | bytes 1048592 | tf_op jit(solution)/shard_map/psum | solution.py:102
  728.7 2.3 copy.23
  (9 shorter events, 0.1 us)
Async XLA Ops:
  7.2 63.1 %copy-start = (bf16[512,512]{1,0:T(8,128)(2,1)S(1)}, bf16[512,512]{1,0:T(8,128)(2,1)}, u32[]{:S(2)}) copy-start(bf16[512,512]{1,0:T(8,128)(2,1)} %param.15) | copy-start | bytes 1572868
  7.2 12.8 %copy-start.5 = (s32[2,2]{1,0:T(2,128)S(1)}, s32[2,2]{1,0:T(2,128)}, u32[]{:S(2)}) copy-start(s32[2,2]{1,0:T(2,128)} %param.11) | copy-start | bytes 52
  7.2 12.9 %copy-start.8 = (s32[2]{0:T(128)S(1)}, s32[2]{0:T(128)}, u32[]{:S(2)}) copy-start(s32[2]{0:T(128)} %param.13) | copy-start | bytes 28
  7.2 12.9 %copy-start.9 = (s32[2]{0:T(128)S(1)}, s32[2]{0:T(128)}, u32[]{:S(2)}) copy-start(s32[2]{0:T(128)} %param.12) | copy-start | bytes 28
  9.6 31.7 %all-to-all-start = ((bf16[64,16,512]{2,0,1:T(8,128)(2,1)}), bf16[64,16,512]{2,0,1:T(8,128)(2,1)S(1)}, u32[]{:S(2)}, u32[]{:S(2)}) async-start(bf16[64,16,512]{2,0,1:T(8,128)(2,1)} %bitcast.14), calls=%async_computation | async-start | bytes 2097152 | tf_op jit(solution)/shard_map/all_to_all | solution.py:73
  50.4 12.0 %copy-start.6 = (bf16[512]{0:T(512)(128)(2,1)S(1)}, bf16[512]{0:T(512)(128)(2,1)}, u32[]{:S(2)}) copy-start(bf16[512]{0:T(512)(128)(2,1)} %param.14) | copy-start | bytes 3076
  53.5 20.0 %copy-start.1 = (bf16[2048,512]{1,0:T(8,128)(2,1)}, bf16[2048,512]{1,0:T(8,128)(2,1)S(1)}, u32[]{:S(2)}) copy-start(bf16[2048,512]{1,0:T(8,128)(2,1)S(1)} %get-tuple-element.12) | copy-start | bytes 6291460
  54.3 15.8 %all-to-all-start.1 = ((f32[16,1,2048]{2,1,0:T(1,128)}), f32[16,1,2048]{2,1,0:T(1,128)S(1)}, u32[]{:S(2)}, u32[]{:S(2)}) async-start(f32[16,1,2048]{2,1,0:T(1,128)} %broadcast_in_dim.27), calls=%async_computation.1 | async-start | bytes 262144 | tf_op jit(solution)/shard_map/all_to_all | solution.py:14
  62.4 105.3 %reduce-scatter.2.cloned.1.call-start = ((), (), s32[]{:S(2)}) async-start(), calls=%async_computation.4 | async-start | bytes 4456448 | tf_op jit(solution)/shard_map/reduce_scatter | solution.py:83
  73.5 0.7 copy-start.7
  73.5 94.1 %copy-start.4 = (bf16[128,512]{1,0:T(8,128)(2,1)S(1)}, bf16[128,512]{1,0:T(8,128)(2,1)}, u32[]{:S(2)}) copy-start(bf16[128,512]{1,0:T(8,128)(2,1)} %param.17) | copy-start | bytes 393220
  73.6 655.1 %all-reduce.3.cloned.1.call-start = ((), (), s32[]{:S(2)}) async-start(), calls=%async_computation.5 | async-start | bytes 2097152 | tf_op jit(solution)/shard_map/psum | solution.py:102
  169.5 46.6 %copy-start.2 = (bf16[2048,512]{1,0:T(8,128)(2,1)S(1)}, bf16[2048,512]{1,0:T(8,128)(2,1)}, u32[]{:S(2)}) copy-start(bf16[2048,512]{1,0:T(8,128)(2,1)} %copy-done.1) | copy-start | bytes 6291460
  218.6 1.6 copy-start.3
Sparse Core Ops, SparseCore 0:
  73.7 93.8 reduce-scatter.1
  218.7 509.9 all-reduce.2
where the time goes:
time: 738 us
  waiting for transfers between devices  497 us (67%)
  blocking collectives  179 us (24%)
  starting transfers between devices  18.5 us (3%)
  local copies, waits for them, and re-layouts  16.7 us (2%)
  between operations  14.3 us (2%)
    psum x1, waiting for transfers between devices, on_device(): lax.psum((weight_local, bias_local, gain_local), 'grp')  375 us
    psum x1, blocking collectives, on_device(): lax.psum((weight_local, bias_local, gain_local), 'grp')  132 us
    reduce_scatter x1, waiting for transfers between devices, on_device(): lax.psum_scatter(jnp.dot(normed, key_weight, preferred_element_type=jnp.f...  93.3 us
    all_to_all x1, blocking collectives, copy_for_each(): lax.all_to_all(jnp.broadcast_to(value[None], (devices, *value.shape)), ax...  46.6 us
    all_to_all x1, waiting for transfers between devices, on_device(): lax.all_to_all(image_embeds, 'tp', split_axis=1, concat_axis=0, tiled=True)  20.9 us
  transfers between devices with their start and end apart: 4, of which 4 were waited for; matrix products, arithmetic and copies ran while one was open for 0% of the time, Pallas kernels for 0%

commit v1 on v0

v1 whole, which is shorter than its diff:
```python
import jax
import jax.numpy as jnp
from jax import lax
from jax.experimental import pallas as pl
from jax.experimental.pallas import tpu as pltpu
from jax.sharding import Mesh
from jax.sharding import PartitionSpec as P

D = 8192
PATCH = 256
LEN = 1024
EPS = 1e-06
BF = jnp.bfloat16
F32 = jnp.float32
AXES = ("zh", "y", "c", "zl", "x")
SIZES = (3, 8, 2, 4, 4)
GRP = ("zh", "y", "c")
TP = ("zl", "x")
RING = ("zh", "y")
PIECES = 24
SLAB = 48
HALF = PIECES * SLAB
MIB = 1024 * 1024


def call(kernel, outs, args, smem=0, scratch=(), flops=0, nbytes=0, mib=12):
    in_specs = [pl.BlockSpec(memory_space=pltpu.SMEM)] * smem
    in_specs += [pl.BlockSpec(memory_space=pltpu.VMEM)] * (len(args) - smem)
    many = isinstance(outs, (list, tuple))
    vmem = pl.BlockSpec(memory_space=pltpu.VMEM)
    return pl.pallas_call(
        kernel,
        out_shape=outs,
        in_specs=in_specs,
        out_specs=[vmem] * len(outs) if many else vmem,
        scratch_shapes=list(scratch),
        cost_estimate=pl.CostEstimate(flops=flops, bytes_accessed=nbytes, transcendentals=0),
        compiler_params=pltpu.CompilerParams(vmem_limit_bytes=mib * MIB),
    )(*args)


def shape(dims, dtype):
    return jax.ShapeDtypeStruct(dims, dtype)


def own_valid(length_ref, rows, lanes):
    zl, x = lax.axis_index("zl"), lax.axis_index("x")
    position = (zl % 2) * 512 + x * 128 + lax.broadcasted_iota(jnp.int32, (rows, lanes), 0)
    return (position < length_ref[zl // 2]).astype(F32)


def mask_kernel(length_ref, cot_ref, out_ref):
    out_ref[...] = (cot_ref[...].astype(F32) * own_valid(length_ref, 128, 512)).astype(BF)


def prep_kernel(text_ref, image_ref, out_ref):
    rows = image_ref.shape[0]
    total = jnp.zeros((rows, 512), F32)
    for t in range(16):
        part = image_ref[:, t * 512 : (t + 1) * 512].astype(F32)
        total = total + part * part
    rstd = lax.rsqrt(jnp.sum(total, axis=1, keepdims=True) / D + EPS)
    row = lax.broadcasted_iota(jnp.int32, (8, 512), 0)
    ones = jnp.ones((8, 128), F32)
    parts = jnp.zeros((8, 512), F32)
    for j in range(4):
        lanes = jnp.zeros((512, 128), F32)
        for b in range(4):
            part = text_ref[j * 512 : (j + 1) * 512, b * 128 : (b + 1) * 128].astype(F32)
            lanes = lanes + part * part
        sums = lax.dot_general(
            ones, lanes, (((1,), (1,)), ((), ())), precision=lax.Precision.HIGHEST,
            preferred_element_type=F32,
        )
        top = sums.astype(BF).astype(F32)
        parts = parts + jnp.where(row == j, top, 0.0) + jnp.where(row == j + 4, sums - top, 0.0)
    parts = parts.astype(BF)
    for t in range(16):
        part = image_ref[:, t * 512 : (t + 1) * 512].astype(F32)
        out_ref[t, :64, :] = (part * rstd).astype(BF)
        out_ref[t, 64:, :] = parts


def block(z, q):
    return pl.ds(pl.multiple_of((z * 4 + q) * 128, 128), 128)


def norm_kernel(
    offset_ref, count_ref, text_ref, got_ref, weight_ref, gain_ref, normed_ref, key0_ref, key1_ref, key2_ref, key3_ref
):
    squares = jnp.concatenate([got_ref[t, 64:, :] for t in range(16)], axis=0)
    pick = lax.broadcasted_iota(jnp.int32, (128, 128), 0) % 4
    gain = gain_ref[...].astype(F32)
    for seq in range(2):
        images = jnp.concatenate([got_ref[seq * 8 + t, :64, :] for t in range(8)], axis=0)
        for part in range(4):
            base = part * 256
            ones = (pick == seq * 2 + part // 2).astype(F32).astype(BF)
            cols = slice((part % 2) * 256, (part % 2) * 256 + 256)
            total = lax.dot_general(
                squares[:, cols], ones, (((0,), (0,)), ((), ())), preferred_element_type=F32
            )
            position = base + lax.broadcasted_iota(jnp.int32, (256, 256), 0)
            column = lax.broadcasted_iota(jnp.int32, (256, 256), 1)
            narrow = base + lax.broadcasted_iota(jnp.int32, (256, 128), 0)
            hot, covered = [], None
            for slot in range(2):
                start = jnp.where(slot < count_ref[seq], offset_ref[seq, slot], LEN)
                hot.append((position - start == column).astype(F32).astype(BF))
                here = (narrow >= start) & (narrow < start + PATCH)
                covered = here if covered is None else covered | here
            scale = jnp.where(covered, 1.0, lax.rsqrt(total / D + EPS))
            placed = jnp.dot(hot[0], images[:256], preferred_element_type=F32)
            placed = placed + jnp.dot(hot[1], images[256:], preferred_element_type=F32)
            rows = slice(seq * LEN + base, seq * LEN + base + 256)
            for b in range(4):
                cols = slice(b * 128, (b + 1) * 128)
                text = text_ref[rows, cols].astype(F32)
                value = jnp.where(covered, placed[:, cols], text) * scale * gain[:, cols]
                normed_ref[rows, cols] = value.astype(BF)
    x = lax.axis_index("x")
    for s, key_ref in enumerate((key0_ref, key1_ref, key2_ref, key3_ref)):
        q = lax.rem(x + s, 4)
        normed = jnp.concatenate([normed_ref[block(z, q), :] for z in range(4)], axis=0)
        product = jnp.dot(normed, weight_ref[...], preferred_element_type=F32)
        key_ref[...] = product.astype(key_ref.dtype)


def grad_kernel(normed_ref, own_ref, got1_ref, got2_ref, got3_ref, mine_ref, other_ref, grad_ref):
    x, zl, core = lax.axis_index("x"), lax.axis_index("zl"), lax.axis_index("c")
    bias = jnp.zeros((8, 512), F32)
    for s, source in enumerate((own_ref, got1_ref, got2_ref, got3_ref)):
        q = lax.rem(x - s + 4, 4)
        normed = jnp.concatenate([normed_ref[block(lax.rem(zl - i + 4, 4), q), :] for i in range(4)], axis=0)
        masked = source[...]
        part = lax.dot_general(normed, masked, (((0,), (0,)), ((), ())), preferred_element_type=F32)
        grad_ref[...] = part if s == 0 else grad_ref[...] + part
        bias = bias + jnp.dot(jnp.ones((8, 512), BF), masked, preferred_element_type=F32)
    near = pl.ds(pl.multiple_of(core * 256, 256), 256)
    far = pl.ds(pl.multiple_of((1 - core) * 256, 256), 256)
    for b in range(4):
        cols = slice(b * 128, (b + 1) * 128)
        mine_ref[b * 256 : (b + 1) * 256, :] = grad_ref[near, cols]
        other_ref[b * 256 : (b + 1) * 256, :] = grad_ref[far, cols].astype(BF)
    row = lax.broadcasted_iota(jnp.int32, (8, 128), 0)
    packed = jnp.zeros((8, 128), F32)
    for b in range(4):
        packed = packed + jnp.where(row == b, bias[:, b * 128 : (b + 1) * 128], 0.0)
    tail = jnp.concatenate([packed, jnp.zeros((HALF - 1032, 128), F32)], axis=0)
    mine_ref[1024:, :] = tail
    other_ref[1024:, :] = tail.astype(BF)


def piece_kernel(got_ref, out_ref):
    total = got_ref[0].astype(F32)
    for i in range(1, PIECES):
        total = total + got_ref[i].astype(F32)
    total = total.astype(BF)
    for i in range(PIECES):
        out_ref[i] = total


def final_kernel(mine_ref, other_ref, weight_ref, gain_ref, grad_ref, bias_ref, gain_grad_ref):
    core = lax.axis_index("c")
    near = pl.ds(pl.multiple_of(core * 256, 256), 256)
    far = pl.ds(pl.multiple_of((1 - core) * 256, 256), 256)
    for b in range(4):
        cols = slice(b * 128, (b + 1) * 128)
        rows = slice(b * 256, (b + 1) * 256)
        grad_ref[near, cols] = mine_ref[rows, :].astype(F32)
        grad_ref[far, cols] = other_ref[rows, :].astype(F32)
    lanes = jnp.zeros((512, 128), F32)
    for b in range(4):
        cols = slice(b * 128, (b + 1) * 128)
        lanes = lanes + grad_ref[:, cols] * weight_ref[:, cols].astype(F32)
    sums = lax.dot_general(
        jnp.ones((8, 128), F32), lanes, (((1,), (1,)), ((), ())), precision=lax.Precision.HIGHEST,
        preferred_element_type=F32,
    )
    gain_grad_ref[...] = sums[0:1, :] / gain_ref[...].astype(F32)
    tail = mine_ref[1024:1040, :].astype(F32)
    row = lax.broadcasted_iota(jnp.int32, (16, 128), 0)
    for b in range(4):
        bias_ref[:, b * 128 : (b + 1) * 128] = jnp.sum(jnp.where(row == b, tail, 0.0), axis=0, keepdims=True)


def key_sum_kernel(own_ref, a_ref, b_ref, c_ref, out0_ref, out1_ref, out2_ref, out3_ref):
    zl = lax.axis_index("zl")
    for s, out_ref in enumerate((out0_ref, out1_ref, out2_ref, out3_ref)):
        rows = pl.ds(pl.multiple_of(lax.rem(zl + s, 4) * 128, 128), 128)
        total = own_ref[rows, :] + a_ref[rows, :].astype(F32)
        total = total + b_ref[rows, :].astype(F32) + c_ref[rows, :].astype(F32)
        out_ref[...] = total.astype(out_ref.dtype)


def key_kernel(length_ref, own_ref, a_ref, b_ref, c_ref, bias_ref, out_ref):
    total = own_ref[...] + a_ref[...].astype(F32) + b_ref[...].astype(F32) + c_ref[...].astype(F32)
    total = (total + bias_ref[...].astype(F32)) * own_valid(length_ref, 128, 512)
    out_ref[...] = total.astype(BF)


def shift(value, axis, by):
    n = lax.axis_size(axis)
    return lax.ppermute(value, axis, [(i, (i + by) % n) for i in range(n)])


def on_device(text, image, offsets, counts, lengths, gain, weight, key_bias, cot):
    gain = gain.reshape(1, 512)
    own = call(mask_kernel, shape((128, 512), BF), (lengths, cot), smem=1, flops=10**6, nbytes=3 * 10**5)
    column = [own] + [shift(own, "zl", s) for s in (1, 2, 3)]
    split = call(prep_kernel, shape((16, 72, 512), BF), (text, image), flops=10**7, nbytes=5 * 10**6)
    images = lax.all_to_all(split, TP, 0, 0, tiled=True)
    column = jnp.concatenate(column, axis=0)
    got = [shift(column, "x", s) for s in (1, 2, 3)]
    normed, key0, *keys = call(
        norm_kernel,
        [shape((2048, 512), BF), shape((512, 512), F32)] + [shape((512, 512), BF)] * 3,
        (offsets, counts, text, images, weight, gain),
        smem=2,
        flops=3 * 10**9,
        nbytes=8 * 10**6,
    )
    keys = [shift(k, "x", s + 1) for s, k in enumerate(keys)]
    mine, other = call(
        grad_kernel,
        [shape((HALF, 128), F32), shape((HALF, 128), BF)],
        (normed, column, *got),
        scratch=[pltpu.VMEM((512, 512), F32)],
        flops=10**9,
        nbytes=5 * 10**6,
    )
    far = shift(other, "c", 1)
    pieces = (mine + far.astype(F32)).astype(BF).reshape(PIECES, SLAB, 128)
    pieces = lax.all_to_all(pieces, RING, 0, 0, tiled=True)
    copies = call(piece_kernel, shape((PIECES, SLAB, 128), BF), (pieces,), flops=10**6, nbytes=10**6)
    half = lax.all_to_all(copies, RING, 0, 0, tiled=True).reshape(HALF, 128)
    sums = call(
        key_sum_kernel,
        [shape((128, 512), F32)] + [shape((128, 512), BF)] * 3,
        (key0, *keys),
        flops=10**6,
        nbytes=4 * 10**6,
    )
    parts = [shift(k, "zl", s + 1) for s, k in enumerate(sums[1:])]
    key_states = call(
        key_kernel,
        shape((128, 512), BF),
        (lengths, sums[0], *parts, key_bias.reshape(1, 512)),
        smem=1,
        flops=10**6,
        nbytes=10**6,
    )
    rest = shift(half, "c", 1)
    weight_grad, bias_grad, gain_grad = call(
        final_kernel,
        [shape((512, 512), F32), shape((1, 512), F32), shape((1, 512), F32)],
        (half, rest, weight, gain),
        flops=10**7,
        nbytes=2 * 10**6,
    )
    return key_states, weight_grad, bias_grad.reshape(512), gain_grad.reshape(512)


def solution(mesh):
    fine = Mesh(mesh.devices.reshape(SIZES), AXES)
    rows = P(GRP + TP, None)
    placed = (P(GRP, TP), rows, P(GRP, None), P(GRP), P(GRP), P(TP), P(TP, None), P(), rows)
    return jax.shard_map(
        on_device,
        mesh=fine,
        in_specs=placed,
        out_specs=(rows, P(TP, None), P(), P(TP)),
        check_vma=False,
    )
```

time: 738 us -> 183 us (0.25)
  waiting for transfers between devices: 497 us -> 65.7 us
  blocking collectives: 179 us -> 33.8 us
  starting transfers between devices: 18.5 us -> 61.8 us
  Pallas kernels: 0 us -> 13.8 us
  between operations: 14.3 us -> 0.97 us
  local copies, waits for them, and re-layouts: 16.7 us -> 3.84 us
    psum x1 -> x0, waiting for transfers between devices: 375 us -> none  [on_device(): lax.psum((weight_local, bias_local, gain_local), 'grp')]
    psum x1 -> x0, blocking collectives: 132 us -> none  [on_device(): lax.psum((weight_local, bias_local, gain_local), 'grp')]
    reduce_scatter x1 -> x0, waiting for transfers between devices: 93.3 us -> none  [on_device(): lax.psum_scatter(jnp.dot(normed, key_weight, preferred_element_type=jnp.f...]
    ppermute x0 -> x14, waiting for transfers between devices: none -> 59.5 us  [shift(): return lax.ppermute(value, axis, [(i, (i + by) % n) for i in range(n)])]
    ppermute x0 -> x14, starting transfers between devices: none -> 45.1 us  [shift(): return lax.ppermute(value, axis, [(i, (i + by) % n) for i in range(n)])]
    all_to_all x2, waiting for transfers between devices: 28.6 us -> 6.17 us  [the longest x1 6.17 us: on_device(): half = lax.all_to_all(copies, RING, 0, 0, tiled=True).reshape(HALF, 128)]
    pallas_call x0 -> x8, Pallas kernels: none -> 13.8 us  [call(): pl.pallas_call(kernel, out_shape=outs, in_specs=in_specs, out_specs=[vmem...]
    all_to_all x1, blocking collectives: 46.6 us -> 33.8 us  [on_device(): pieces = lax.all_to_all(pieces, RING, 0, 0, tiled=True)]
  transfers between devices with their start and end apart: 4 -> 16, of which waited for: 4 -> 9; matrix products, arithmetic and copies ran while one was open for 0% -> 0% of each run, Pallas kernels for 0% -> 4%
where the time goes in v1:
time: 183 us; the launch traced here: 180 us
  waiting for transfers between devices  65.7 us (36%)
  starting transfers between devices  61.8 us (34%)
  blocking collectives  33.8 us (18%)
  Pallas kernels  13.8 us (8%)
  local copies, waits for them, and re-layouts  3.84 us (2%)
    ppermute x14, waiting for transfers between devices, shift(): return lax.ppermute(value, axis, [(i, (i + by) % n) for i in range(n)])  59.5 us
    ppermute x14, starting transfers between devices, shift(): return lax.ppermute(value, axis, [(i, (i + by) % n) for i in range(n)])  45.1 us
    all_to_all x1, blocking collectives, on_device(): pieces = lax.all_to_all(pieces, RING, 0, 0, tiled=True)  33.8 us
    pallas_call x8, Pallas kernels, call(): pl.pallas_call(kernel, out_shape=outs, in_specs=in_specs, out_specs=[vmem...  13.8 us
    all_to_all x1, starting transfers between devices, on_device(): images = lax.all_to_all(split, TP, 0, 0, tiled=True)  10.7 us
    all_to_all x1, waiting for transfers between devices, on_device(): half = lax.all_to_all(copies, RING, 0, 0, tiled=True).reshape(HALF, 128)  6.17 us
    all_to_all x1, starting transfers between devices, on_device(): half = lax.all_to_all(copies, RING, 0, 0, tiled=True).reshape(HALF, 128)  5.98 us
    unnamed x30, local copies, waits for them, and re-layouts  3.83 us
  transfers between devices with their start and end apart: 16, of which 9 were waited for; matrix products, arithmetic and copies ran while one was open for 0% of the time, Pallas kernels for 4%

profile of v1, /device:TPU:1, one launch (start us, length us, event | category | flops | bytes accessed | tf_op | source)
XLA Modules:
  0.0 180.1 jit_solution(13672162485524265554)
XLA Ops:
  0.6 0.0 copy-start
  0.6 1.6 copy-done
  2.2 1.2 copy-done.4
  3.5 2.3 %shard_map.120 = bf16[16,72,512]{2,1,0:T(8,128)(2,1)} custom-call(bf16[2048,512]{1,0:T(8,128)(2,1)S(1)} %copy-done, bf16[64,8192]{1,0:T(8,128)(2,1)S(1)} %copy-done.4), custom_call_target="tpu_custom_call" | custom-call | flops 10000000 | bytes 5000000 | tf_op jit(solution)/shard_map/pallas_call | solution.py:31
  5.8 0.0 copy-start.12
  5.8 10.7 %all-to-all-start = ((bf16[16,72,512]{2,1,0:T(8,128)(2,1)}), bf16[16,72,512]{2,1,0:T(8,128)(2,1)}, u32[]{:S(2)}, u32[]{:S(2)}) async-start(bf16[16,72,512]{2,1,0:T(8,128)(2,1)} %shard_map.120), calls=%async_computation | async-start | bytes 2359296 | tf_op jit(solution)/shard_map/all_to_all | solution.py:212
  16.5 0.6 shard_map.124
  17.1 5.0 %collective-permute-start.8 = (bf16[128,512]{1,0:T(8,128)(2,1)S(1)}, bf16[128,512]{1,0:T(8,128)(2,1)S(1)}, u32[]{:S(2)}, u32[]{:S(2)}) collective-permute-start(bf16[128,512]{1,0:T(8,128)(2,1)S(1)} %shard_map.124), channel_id=1, source_target_pairs={{0,12},{4,0},{8,4},{12,8},{1,13},{5,1},{9,5},{13,9},{2,14},{6,2},{... | collective-permute-start | bytes 393224 | tf_op jit(solution)/shard_map/ppermute | solution.py:204
  22.1 1.9 %collective-permute-start.7 = (bf16[128,512]{1,0:T(8,128)(2,1)S(1)}, bf16[128,512]{1,0:T(8,128)(2,1)S(1)}, u32[]{:S(2)}, u32[]{:S(2)}) collective-permute-start(bf16[128,512]{1,0:T(8,128)(2,1)S(1)} %shard_map.124), channel_id=1, source_target_pairs={{0,8},{4,12},{8,0},{12,4},{1,9},{5,13},{9,1},{13,5},{2,10},{6,14},... | collective-permute-start | bytes 393224 | tf_op jit(solution)/shard_map/ppermute | solution.py:204
  24.0 2.5 %collective-permute-start.6 = (bf16[128,512]{1,0:T(8,128)(2,1)S(1)}, bf16[128,512]{1,0:T(8,128)(2,1)S(1)}, u32[]{:S(2)}, u32[]{:S(2)}) collective-permute-start(bf16[128,512]{1,0:T(8,128)(2,1)S(1)} %shard_map.124), channel_id=1, source_target_pairs={{0,4},{4,8},{8,12},{12,0},{1,5},{5,9},{9,13},{13,1},{2,6},{6,10},{... | collective-permute-start | bytes 393224 | tf_op jit(solution)/shard_map/ppermute | solution.py:204
  26.5 7.8 %collective-permute-done.8 = bf16[128,512]{1,0:T(8,128)(2,1)S(1)} collective-permute-done((bf16[128,512]{1,0:T(8,128)(2,1)S(1)}, bf16[128,512]{1,0:T(8,128)(2,1)S(1)}, u32[]{:S(2)}, u32[]{:S(2)}) %collective-permute-start.8) | collective-permute-done | bytes 131104 | tf_op jit(solution)/shard_map/ppermute | solution.py:204
  34.3 20.5 %collective-permute-done.7 = bf16[128,512]{1,0:T(8,128)(2,1)S(1)} collective-permute-done((bf16[128,512]{1,0:T(8,128)(2,1)S(1)}, bf16[128,512]{1,0:T(8,128)(2,1)S(1)}, u32[]{:S(2)}, u32[]{:S(2)}) %collective-permute-start.7) | collective-permute-done | bytes 131104 | tf_op jit(solution)/shard_map/ppermute | solution.py:204
  54.8 0.0 collective-permute-done.6
  54.8 3.1 %collective-permute-start.9 = (bf16[512,512]{1,0:T(8,128)(2,1)S(1)}, bf16[512,512]{1,0:T(8,128)(2,1)}, u32[]{:S(2)}, u32[]{:S(2)}) collective-permute-start(bf16[512,512]{1,0:T(8,128)(2,1)S(1)} %pad_maximum_fusion.own_ref), channel_id=1, source_target_pairs={{0,1},{1,2},{2,3},{3,0},{4,5},{5,6},{6,7},{7,4},{8,9},{9,10},{10,1... | collective-permute-start | bytes 1572872 | tf_op jit(solution)/shard_map/ppermute | solution.py:204
  57.9 3.6 %collective-permute-start.10 = (bf16[512,512]{1,0:T(8,128)(2,1)S(1)}, bf16[512,512]{1,0:T(8,128)(2,1)}, u32[]{:S(2)}, u32[]{:S(2)}) collective-permute-start(bf16[512,512]{1,0:T(8,128)(2,1)S(1)} %pad_maximum_fusion.own_ref), channel_id=1, source_target_pairs={{0,2},{1,3},{2,0},{3,1},{4,6},{5,7},{6,4},{7,5},{8,10},{9,11},{10,... | collective-permute-start | bytes 1572872 | tf_op jit(solution)/shard_map/ppermute | solution.py:204
  61.5 3.1 %collective-permute-start.11 = (bf16[512,512]{1,0:T(8,128)(2,1)S(1)}, bf16[512,512]{1,0:T(8,128)(2,1)}, u32[]{:S(2)}, u32[]{:S(2)}) collective-permute-start(bf16[512,512]{1,0:T(8,128)(2,1)S(1)} %pad_maximum_fusion.own_ref), channel_id=1, source_target_pairs={{0,3},{1,0},{2,1},{3,2},{4,7},{5,4},{6,5},{7,6},{8,11},{9,8},{10,9... | collective-permute-start | bytes 1572872 | tf_op jit(solution)/shard_map/ppermute | solution.py:204
  64.6 0.0 all-to-all-done.got_ref
  64.7 4.4 %shard_map.121 = (bf16[2048,512]{1,0:T(8,128)(2,1)S(1)}, f32[512,512]{1,0:T(8,128)S(1)}, bf16[512,512]{1,0:T(8,128)(2,1)S(1)}, bf16[512,512]{1,0:T(8,128)(2,1)S(1)}, bf16[512,512]{1,0:T(8,128)(2,1)S(1)}) custom-call(s32[2,2]{1,0:T(2,128)S(1)} %copy-done.11, s32[2]{0:T(128)S(1)} %copy-done.12, bf16[2048,512]{1,0:T(8,128)(2,1)S(1)} %copy-done.1, ...), custom_call_target="tpu_custom_call" | custom-call | flops 3000000000 | bytes 8000000 | tf_op jit(solution)/shard_map/pallas_call | solution.py:31
  69.1 0.0 copy-start.2
  69.1 1.0 copy-done.2
  70.1 0.0 collective-permute-done.9.got1_ref
  70.1 9.7 %collective-permute-done.10.got2_ref = bf16[512,512]{1,0:T(8,128)(2,1)} collective-permute-done((bf16[512,512]{1,0:T(8,128)(2,1)S(1)}, bf16[512,512]{1,0:T(8,128)(2,1)}, u32[]{:S(2)}, u32[]{:S(2)}) %collective-permute-start.10) | collective-permute-done | bytes 524320 | tf_op jit(solution)/shard_map/ppermute | solution.py:204
  79.8 4.7 %collective-permute-done.11.got3_ref = bf16[512,512]{1,0:T(8,128)(2,1)} collective-permute-done((bf16[512,512]{1,0:T(8,128)(2,1)S(1)}, bf16[512,512]{1,0:T(8,128)(2,1)}, u32[]{:S(2)}, u32[]{:S(2)}) %collective-permute-start.11) | collective-permute-done | bytes 524320 | tf_op jit(solution)/shard_map/ppermute | solution.py:204
  84.5 3.0 %shard_map.125 = (f32[1152,128]{1,0:T(8,128)S(1)}, bf16[1152,128]{1,0:T(8,128)(2,1)S(1)}) custom-call(bf16[2048,512]{1,0:T(8,128)(2,1)S(1)} %get-tuple-element.26.normed_ref, bf16[512,512]{1,0:T(8,128)(2,1)S(1)} %pad_maximum_fusion.own_ref, bf16[512,512]{1,0:T(8,128)(2,1)} %collective-permute-done.9.got1_ref, ...), custom_call_target="tpu_custom_call" | custom-call | flops 1000000000 | bytes 5000000 | tf_op jit(solution)/shard_map/pallas_call | solution.py:31
  87.5 0.0 copy-start.3
  87.5 3.7 %collective-permute-start.12 = (bf16[1152,128]{1,0:T(8,128)(2,1)S(1)}, bf16[1152,128]{1,0:T(8,128)(2,1)S(1)}, u32[]{:S(2)}, u32[]{:S(2)}) collective-permute-start(bf16[1152,128]{1,0:T(8,128)(2,1)S(1)} %get-tuple-element.28), channel_id=1, source_target_pairs={{0,16},{16,0},{1,17},{17,1},{2,18},{18,2},{3,19},{19,3},{4,20},{20... | collective-permute-start | bytes 884744 | tf_op jit(solution)/shard_map/ppermute | solution.py:204
  91.2 1.2 collective-permute-done.12
  92.4 0.1 add_convert_fusion
  92.5 0.0 copy-start.14
  92.5 33.8 %all_to_all.15.got_ref = bf16[24,48,128]{2,1,0:T(8,128)(2,1)S(1)} all-to-all(bf16[24,48,128]{2,1,0:T(8,128)(2,1)S(1)} %bitcast.6), channel_id=1, replica_groups=mesh['zh'=3,'y'=8,'c'=2,'zl'=4,'x'=4] {'zh','y'}, dimensions={0} | all-to-all | bytes 589824 | tf_op jit(solution)/shard_map/all_to_all | solution.py:234
  126.4 0.8 shard_map.126
  127.1 6.0 %all-to-all-start.2 = ((bf16[24,48,128]{2,1,0:T(8,128)(2,1)}), bf16[24,48,128]{2,1,0:T(8,128)(2,1)S(1)}, u32[]{:S(2)}, u32[]{:S(2)}) async-start(bf16[24,48,128]{2,1,0:T(8,128)(2,1)} %shard_map.126), calls=%async_computation.2 | async-start | bytes 589824 | tf_op jit(solution)/shard_map/all_to_all | solution.py:236
  133.1 3.8 %collective-permute-start = (bf16[512,512]{1,0:T(8,128)(2,1)}, bf16[512,512]{1,0:T(8,128)(2,1)S(1)}, u32[]{:S(2)}, u32[]{:S(2)}) collective-permute-start(bf16[512,512]{1,0:T(8,128)(2,1)} %copy-done.10), channel_id=1, source_target_pairs={{0,1},{1,2},{2,3},{3,0},{4,5},{5,6},{6,7},{7,4},{8,9},{9,10},{10,1... | collective-permute-start | bytes 1572872 | tf_op jit(solution)/shard_map/ppermute | solution.py:204
  136.9 3.5 %collective-permute-start.1 = (bf16[512,512]{1,0:T(8,128)(2,1)}, bf16[512,512]{1,0:T(8,128)(2,1)S(1)}, u32[]{:S(2)}, u32[]{:S(2)}) collective-permute-start(bf16[512,512]{1,0:T(8,128)(2,1)} %copy-done.9), channel_id=1, source_target_pairs={{0,2},{1,3},{2,0},{3,1},{4,6},{5,7},{6,4},{7,5},{8,10},{9,11},{10,... | collective-permute-start | bytes 1572872 | tf_op jit(solution)/shard_map/ppermute | solution.py:204
  140.5 3.0 %collective-permute-start.2 = (bf16[512,512]{1,0:T(8,128)(2,1)}, bf16[512,512]{1,0:T(8,128)(2,1)S(1)}, u32[]{:S(2)}, u32[]{:S(2)}) collective-permute-start(bf16[512,512]{1,0:T(8,128)(2,1)} %copy-done.8), channel_id=1, source_target_pairs={{0,3},{1,0},{2,1},{3,2},{4,7},{5,4},{6,5},{7,6},{8,11},{9,8},{10,9... | collective-permute-start | bytes 1572872 | tf_op jit(solution)/shard_map/ppermute | solution.py:204
  143.5 6.2 %all-to-all-done.2 = bf16[24,48,128]{2,1,0:T(8,128)(2,1)S(1)} async-done(((bf16[24,48,128]{2,1,0:T(8,128)(2,1)}), bf16[24,48,128]{2,1,0:T(8,128)(2,1)S(1)}, u32[]{:S(2)}, u32[]{:S(2)}) %all-to-all-start.2) | async-done | bytes 294944 | tf_op jit(solution)/shard_map/all_to_all | solution.py:236
  149.7 2.9 %collective-permute-start.13 = (bf16[1152,128]{1,0:T(8,128)(2,1)S(1)}, bf16[1152,128]{1,0:T(8,128)(2,1)S(1)}, u32[]{:S(2)}, u32[]{:S(2)}) collective-permute-start(bf16[1152,128]{1,0:T(8,128)(2,1)S(1)} %bitcast.4), channel_id=1, source_target_pairs={{0,16},{16,0},{1,17},{17,1},{2,18},{18,2},{3,19},{19,3},{4,20},{20... | collective-permute-start | bytes 884744 | tf_op jit(solution)/shard_map/ppermute | solution.py:204
  152.6 0.0 collective-permute-done.a_ref
  152.6 8.4 %collective-permute-done.1.b_ref = bf16[512,512]{1,0:T(8,128)(2,1)S(1)} collective-permute-done((bf16[512,512]{1,0:T(8,128)(2,1)}, bf16[512,512]{1,0:T(8,128)(2,1)S(1)}, u32[]{:S(2)}, u32[]{:S(2)}) %collective-permute-start.1) | collective-permute-done | bytes 524320 | tf_op jit(solution)/shard_map/ppermute | solution.py:204
  160.9 2.1 %collective-permute-done.2.c_ref = bf16[512,512]{1,0:T(8,128)(2,1)S(1)} collective-permute-done((bf16[512,512]{1,0:T(8,128)(2,1)}, bf16[512,512]{1,0:T(8,128)(2,1)S(1)}, u32[]{:S(2)}, u32[]{:S(2)}) %collective-permute-start.2) | collective-permute-done | bytes 524320 | tf_op jit(solution)/shard_map/ppermute | solution.py:204
  163.1 0.2 shard_map.122
  163.3 1.9 %collective-permute-start.3 = (bf16[128,512]{1,0:T(8,128)(2,1)S(1)}, bf16[128,512]{1,0:T(8,128)(2,1)S(1)}, u32[]{:S(2)}, u32[]{:S(2)}) collective-permute-start(bf16[128,512]{1,0:T(8,128)(2,1)S(1)} %get-tuple-element.23), channel_id=1, source_target_pairs={{0,4},{4,8},{8,12},{12,0},{1,5},{5,9},{9,13},{13,1},{2,6},{6,10},{... | collective-permute-start | bytes 393224 | tf_op jit(solution)/shard_map/ppermute | solution.py:204
  165.2 1.9 %collective-permute-start.4 = (bf16[128,512]{1,0:T(8,128)(2,1)S(1)}, bf16[128,512]{1,0:T(8,128)(2,1)S(1)}, u32[]{:S(2)}, u32[]{:S(2)}) collective-permute-start(bf16[128,512]{1,0:T(8,128)(2,1)S(1)} %get-tuple-element.24), channel_id=1, source_target_pairs={{0,8},{4,12},{8,0},{12,4},{1,9},{5,13},{9,1},{13,5},{2,10},{6,14},... | collective-permute-start | bytes 393224 | tf_op jit(solution)/shard_map/ppermute | solution.py:204
  167.2 5.2 %collective-permute-start.5 = (bf16[128,512]{1,0:T(8,128)(2,1)S(1)}, bf16[128,512]{1,0:T(8,128)(2,1)S(1)}, u32[]{:S(2)}, u32[]{:S(2)}) collective-permute-start(bf16[128,512]{1,0:T(8,128)(2,1)S(1)} %get-tuple-element.25), channel_id=1, source_target_pairs={{0,12},{4,0},{8,4},{12,8},{1,13},{5,1},{9,5},{13,9},{2,14},{6,2},{... | collective-permute-start | bytes 393224 | tf_op jit(solution)/shard_map/ppermute | solution.py:204
  172.4 5.2 %collective-permute-done.4.b_ref = bf16[128,512]{1,0:T(8,128)(2,1)S(1)} collective-permute-done((bf16[128,512]{1,0:T(8,128)(2,1)S(1)}, bf16[128,512]{1,0:T(8,128)(2,1)S(1)}, u32[]{:S(2)}, u32[]{:S(2)}) %collective-permute-start.4) | collective-permute-done | bytes 131104 | tf_op jit(solution)/shard_map/ppermute | solution.py:204
  177.5 0.0 collective-permute-done.5.c_ref
  177.5 1.3 shard_map.123
  178.8 1.2 shard_map.127
  (27 shorter events, 0.1 us)
Async XLA Ops:
  0.6 1.6 copy-start
  2.2 1.2 copy-start.4
  3.5 13.0 %copy-start.6 = (bf16[128,512]{1,0:T(8,128)(2,1)S(1)}, bf16[128,512]{1,0:T(8,128)(2,1)}, u32[]{:S(2)}) copy-start(bf16[128,512]{1,0:T(8,128)(2,1)} %cot_ref.1) | copy-start | bytes 393220
  3.5 13.0 %copy-start.7 = (s32[2]{0:T(128)S(1)}, s32[2]{0:T(128)}, u32[]{:S(2)}) copy-start(s32[2]{0:T(128)} %length_ref.3) | copy-start | bytes 28
  5.7 58.9 %copy-start.13 = (bf16[512]{0:T(512)(128)(2,1)S(1)}, bf16[512]{0:T(512)(128)(2,1)}, u32[]{:S(2)}) copy-start(bf16[512]{0:T(512)(128)(2,1)} %param.14) | copy-start | bytes 3076
  5.7 58.9 %copy-start.1 = (bf16[2048,512]{1,0:T(8,128)(2,1)S(1)}, bf16[2048,512]{1,0:T(8,128)(2,1)}, u32[]{:S(2)}) copy-start(bf16[2048,512]{1,0:T(8,128)(2,1)} %text_ref.3) | copy-start | bytes 6291460
  5.7 58.9 %copy-start.5 = (bf16[512,512]{1,0:T(8,128)(2,1)S(1)}, bf16[512,512]{1,0:T(8,128)(2,1)}, u32[]{:S(2)}) copy-start(bf16[512,512]{1,0:T(8,128)(2,1)} %weight_ref.3) | copy-start | bytes 1572868
  5.8 58.9 %copy-start.11 = (s32[2,2]{1,0:T(2,128)S(1)}, s32[2,2]{1,0:T(2,128)}, u32[]{:S(2)}) copy-start(s32[2,2]{1,0:T(2,128)} %offset_ref.1) | copy-start | bytes 52
  5.8 58.9 %copy-start.12 = (s32[2]{0:T(128)S(1)}, s32[2]{0:T(128)}, u32[]{:S(2)}) copy-start(s32[2]{0:T(128)} %count_ref.1) | copy-start | bytes 28
  5.8 58.9 %all-to-all-start = ((bf16[16,72,512]{2,1,0:T(8,128)(2,1)}), bf16[16,72,512]{2,1,0:T(8,128)(2,1)}, u32[]{:S(2)}, u32[]{:S(2)}) async-start(bf16[16,72,512]{2,1,0:T(8,128)(2,1)} %shard_map.120), calls=%async_computation | async-start | bytes 2359296 | tf_op jit(solution)/shard_map/all_to_all | solution.py:212
  17.1 17.2 %collective-permute-start.8 = (bf16[128,512]{1,0:T(8,128)(2,1)S(1)}, bf16[128,512]{1,0:T(8,128)(2,1)S(1)}, u32[]{:S(2)}, u32[]{:S(2)}) collective-permute-start(bf16[128,512]{1,0:T(8,128)(2,1)S(1)} %shard_map.124), channel_id=1, source_target_pairs={{0,12},{4,0},{8,4},{12,8},{1,13},{5,1},{9,5},{13,9},{2,14},{6,2},{... | collective-permute-start | bytes 393224 | tf_op jit(solution)/shard_map/ppermute | solution.py:204
  22.1 32.7 %collective-permute-start.7 = (bf16[128,512]{1,0:T(8,128)(2,1)S(1)}, bf16[128,512]{1,0:T(8,128)(2,1)S(1)}, u32[]{:S(2)}, u32[]{:S(2)}) collective-permute-start(bf16[128,512]{1,0:T(8,128)(2,1)S(1)} %shard_map.124), channel_id=1, source_target_pairs={{0,8},{4,12},{8,0},{12,4},{1,9},{5,13},{9,1},{13,5},{2,10},{6,14},... | collective-permute-start | bytes 393224 | tf_op jit(solution)/shard_map/ppermute | solution.py:204
  24.0 30.7 %collective-permute-start.6 = (bf16[128,512]{1,0:T(8,128)(2,1)S(1)}, bf16[128,512]{1,0:T(8,128)(2,1)S(1)}, u32[]{:S(2)}, u32[]{:S(2)}) collective-permute-start(bf16[128,512]{1,0:T(8,128)(2,1)S(1)} %shard_map.124), channel_id=1, source_target_pairs={{0,4},{4,8},{8,12},{12,0},{1,5},{5,9},{9,13},{13,1},{2,6},{6,10},{... | collective-permute-start | bytes 393224 | tf_op jit(solution)/shard_map/ppermute | solution.py:204
  54.8 15.3 %collective-permute-start.9 = (bf16[512,512]{1,0:T(8,128)(2,1)S(1)}, bf16[512,512]{1,0:T(8,128)(2,1)}, u32[]{:S(2)}, u32[]{:S(2)}) collective-permute-start(bf16[512,512]{1,0:T(8,128)(2,1)S(1)} %pad_maximum_fusion.own_ref), channel_id=1, source_target_pairs={{0,1},{1,2},{2,3},{3,0},{4,5},{5,6},{6,7},{7,4},{8,9},{9,10},{10,1... | collective-permute-start | bytes 1572872 | tf_op jit(solution)/shard_map/ppermute | solution.py:204
  57.9 21.9 %collective-permute-start.10 = (bf16[512,512]{1,0:T(8,128)(2,1)S(1)}, bf16[512,512]{1,0:T(8,128)(2,1)}, u32[]{:S(2)}, u32[]{:S(2)}) collective-permute-start(bf16[512,512]{1,0:T(8,128)(2,1)S(1)} %pad_maximum_fusion.own_ref), channel_id=1, source_target_pairs={{0,2},{1,3},{2,0},{3,1},{4,6},{5,7},{6,4},{7,5},{8,10},{9,11},{10,... | collective-permute-start | bytes 1572872 | tf_op jit(solution)/shard_map/ppermute | solution.py:204
  61.5 23.0 %collective-permute-start.11 = (bf16[512,512]{1,0:T(8,128)(2,1)S(1)}, bf16[512,512]{1,0:T(8,128)(2,1)}, u32[]{:S(2)}, u32[]{:S(2)}) collective-permute-start(bf16[512,512]{1,0:T(8,128)(2,1)S(1)} %pad_maximum_fusion.own_ref), channel_id=1, source_target_pairs={{0,3},{1,0},{2,1},{3,2},{4,7},{5,4},{6,5},{7,6},{8,11},{9,8},{10,9... | collective-permute-start | bytes 1572872 | tf_op jit(solution)/shard_map/ppermute | solution.py:204
  69.1 1.0 copy-start.2
  70.1 17.4 %copy-start.8 = (bf16[512,512]{1,0:T(8,128)(2,1)}, bf16[512,512]{1,0:T(8,128)(2,1)S(1)}, u32[]{:S(2)}) copy-start(bf16[512,512]{1,0:T(8,128)(2,1)S(1)} %get-tuple-element.21) | copy-start | bytes 1572868
  70.1 22.4 %copy-start.9 = (bf16[512,512]{1,0:T(8,128)(2,1)}, bf16[512,512]{1,0:T(8,128)(2,1)S(1)}, u32[]{:S(2)}) copy-start(bf16[512,512]{1,0:T(8,128)(2,1)S(1)} %get-tuple-element.20) | copy-start | bytes 1572868
  70.1 22.4 %copy-start.10 = (bf16[512,512]{1,0:T(8,128)(2,1)}, bf16[512,512]{1,0:T(8,128)(2,1)S(1)}, u32[]{:S(2)}) copy-start(bf16[512,512]{1,0:T(8,128)(2,1)S(1)} %get-tuple-element.19) | copy-start | bytes 1572868
  87.5 75.6 %copy-start.3 = (f32[512,512]{1,0:T(8,128)S(1)}, f32[512,512]{1,0:T(8,128)}, u32[]{:S(2)}) copy-start(f32[512,512]{1,0:T(8,128)} %copy-done.2) | copy-start | bytes 3145732
  87.5 4.9 %collective-permute-start.12 = (bf16[1152,128]{1,0:T(8,128)(2,1)S(1)}, bf16[1152,128]{1,0:T(8,128)(2,1)S(1)}, u32[]{:S(2)}, u32[]{:S(2)}) collective-permute-start(bf16[1152,128]{1,0:T(8,128)(2,1)S(1)} %get-tuple-element.28), channel_id=1, source_target_pairs={{0,16},{16,0},{1,17},{17,1},{2,18},{18,2},{3,19},{19,3},{4,20},{20... | collective-permute-start | bytes 884744 | tf_op jit(solution)/shard_map/ppermute | solution.py:204
  92.5 79.8 %copy-start.14 = (bf16[512]{0:T(512)(128)(2,1)S(1)}, bf16[512]{0:T(512)(128)(2,1)}, u32[]{:S(2)}) copy-start(bf16[512]{0:T(512)(128)(2,1)} %param.16) | copy-start | bytes 3076
  127.1 22.5 %all-to-all-start.2 = ((bf16[24,48,128]{2,1,0:T(8,128)(2,1)}), bf16[24,48,128]{2,1,0:T(8,128)(2,1)S(1)}, u32[]{:S(2)}, u32[]{:S(2)}) async-start(bf16[24,48,128]{2,1,0:T(8,128)(2,1)} %shard_map.126), calls=%async_computation.2 | async-start | bytes 589824 | tf_op jit(solution)/shard_map/all_to_all | solution.py:236
  133.1 19.4 %collective-permute-start = (bf16[512,512]{1,0:T(8,128)(2,1)}, bf16[512,512]{1,0:T(8,128)(2,1)S(1)}, u32[]{:S(2)}, u32[]{:S(2)}) collective-permute-start(bf16[512,512]{1,0:T(8,128)(2,1)} %copy-done.10), channel_id=1, source_target_pairs={{0,1},{1,2},{2,3},{3,0},{4,5},{5,6},{6,7},{7,4},{8,9},{9,10},{10,1... | collective-permute-start | bytes 1572872 | tf_op jit(solution)/shard_map/ppermute | solution.py:204
  136.9 24.0 %collective-permute-start.1 = (bf16[512,512]{1,0:T(8,128)(2,1)}, bf16[512,512]{1,0:T(8,128)(2,1)S(1)}, u32[]{:S(2)}, u32[]{:S(2)}) collective-permute-start(bf16[512,512]{1,0:T(8,128)(2,1)} %copy-done.9), channel_id=1, source_target_pairs={{0,2},{1,3},{2,0},{3,1},{4,6},{5,7},{6,4},{7,5},{8,10},{9,11},{10,... | collective-permute-start | bytes 1572872 | tf_op jit(solution)/shard_map/ppermute | solution.py:204
  140.5 22.6 %collective-permute-start.2 = (bf16[512,512]{1,0:T(8,128)(2,1)}, bf16[512,512]{1,0:T(8,128)(2,1)S(1)}, u32[]{:S(2)}, u32[]{:S(2)}) collective-permute-start(bf16[512,512]{1,0:T(8,128)(2,1)} %copy-done.8), channel_id=1, source_target_pairs={{0,3},{1,0},{2,1},{3,2},{4,7},{5,4},{6,5},{7,6},{8,11},{9,8},{10,9... | collective-permute-start | bytes 1572872 | tf_op jit(solution)/shard_map/ppermute | solution.py:204
  149.7 29.2 %collective-permute-start.13 = (bf16[1152,128]{1,0:T(8,128)(2,1)S(1)}, bf16[1152,128]{1,0:T(8,128)(2,1)S(1)}, u32[]{:S(2)}, u32[]{:S(2)}) collective-permute-start(bf16[1152,128]{1,0:T(8,128)(2,1)S(1)} %bitcast.4), channel_id=1, source_target_pairs={{0,16},{16,0},{1,17},{17,1},{2,18},{18,2},{3,19},{19,3},{4,20},{20... | collective-permute-start | bytes 884744 | tf_op jit(solution)/shard_map/ppermute | solution.py:204
  163.3 9.0 %collective-permute-start.3 = (bf16[128,512]{1,0:T(8,128)(2,1)S(1)}, bf16[128,512]{1,0:T(8,128)(2,1)S(1)}, u32[]{:S(2)}, u32[]{:S(2)}) collective-permute-start(bf16[128,512]{1,0:T(8,128)(2,1)S(1)} %get-tuple-element.23), channel_id=1, source_target_pairs={{0,4},{4,8},{8,12},{12,0},{1,5},{5,9},{9,13},{13,1},{2,6},{6,10},{... | collective-permute-start | bytes 393224 | tf_op jit(solution)/shard_map/ppermute | solution.py:204
  165.2 12.3 %collective-permute-start.4 = (bf16[128,512]{1,0:T(8,128)(2,1)S(1)}, bf16[128,512]{1,0:T(8,128)(2,1)S(1)}, u32[]{:S(2)}, u32[]{:S(2)}) collective-permute-start(bf16[128,512]{1,0:T(8,128)(2,1)S(1)} %get-tuple-element.24), channel_id=1, source_target_pairs={{0,8},{4,12},{8,0},{12,4},{1,9},{5,13},{9,1},{13,5},{2,10},{6,14},... | collective-permute-start | bytes 393224 | tf_op jit(solution)/shard_map/ppermute | solution.py:204
  167.2 10.4 %collective-permute-start.5 = (bf16[128,512]{1,0:T(8,128)(2,1)S(1)}, bf16[128,512]{1,0:T(8,128)(2,1)S(1)}, u32[]{:S(2)}, u32[]{:S(2)}) collective-permute-start(bf16[128,512]{1,0:T(8,128)(2,1)S(1)} %get-tuple-element.25), channel_id=1, source_target_pairs={{0,12},{4,0},{8,4},{12,8},{1,13},{5,1},{9,5},{13,9},{2,14},{6,2},{... | collective-permute-start | bytes 393224 | tf_op jit(solution)/shard_map/ppermute | solution.py:204

commit v2 on v1

--- a/solution.py
+++ b/solution.py
@@ -1,3 +1,5 @@
+import functools
+
 import jax
 import jax.numpy as jnp
 from jax import lax
@@ -23,7 +25,7 @@
 MIB = 1024 * 1024
 
 
-def call(kernel, outs, args, smem=0, scratch=(), flops=0, nbytes=0, mib=12):
+def call(kernel, outs, args, smem=0, scratch=(), flops=0, nbytes=0, mib=50):
     in_specs = [pl.BlockSpec(memory_space=pltpu.SMEM)] * smem
     in_specs += [pl.BlockSpec(memory_space=pltpu.VMEM)] * (len(args) - smem)
     many = isinstance(outs, (list, tuple))
@@ -50,7 +52,9 @@
 
 
 def mask_kernel(length_ref, cot_ref, out_ref):
-    out_ref[...] = (cot_ref[...].astype(F32) * own_valid(length_ref, 128, 512)).astype(BF)
+    own = (cot_ref[...].astype(F32) * own_valid(length_ref, 128, 512)).astype(BF)
+    for z in range(4):
+        out_ref[z] = own
 
 
 def prep_kernel(text_ref, image_ref, out_ref):
@@ -86,7 +90,7 @@
 
 
 def norm_kernel(
-    offset_ref, count_ref, text_ref, got_ref, weight_ref, gain_ref, normed_ref, key0_ref, key1_ref, key2_ref, key3_ref
+    offset_ref, count_ref, text_ref, got_ref, weight_ref, gain_ref, normed_ref, key1_ref, key2_ref, key3_ref
 ):
     squares = jnp.concatenate([got_ref[t, 64:, :] for t in range(16)], axis=0)
     pick = lax.broadcasted_iota(jnp.int32, (128, 128), 0) % 4
@@ -119,36 +123,31 @@
                 value = jnp.where(covered, placed[:, cols], text) * scale * gain[:, cols]
                 normed_ref[rows, cols] = value.astype(BF)
     x = lax.axis_index("x")
-    for s, key_ref in enumerate((key0_ref, key1_ref, key2_ref, key3_ref)):
-        q = lax.rem(x + s, 4)
+    for s, key_ref in enumerate((key1_ref, key2_ref, key3_ref)):
+        q = lax.rem(x + s + 1, 4)
         normed = jnp.concatenate([normed_ref[block(z, q), :] for z in range(4)], axis=0)
-        product = jnp.dot(normed, weight_ref[...], preferred_element_type=F32)
-        key_ref[...] = product.astype(key_ref.dtype)
-
-
-def grad_kernel(normed_ref, own_ref, got1_ref, got2_ref, got3_ref, mine_ref, other_ref, grad_ref):
-    x, zl, core = lax.axis_index("x"), lax.axis_index("zl"), lax.axis_index("c")
+        key_ref[...] = jnp.dot(normed, weight_ref[...], preferred_element_type=F32).astype(BF)
+
+
+def grad_kernel(far, normed_ref, own_ref, got1_ref, got2_ref, got3_ref, out_ref, grad_ref):
+    x, core = lax.axis_index("x"), lax.axis_index("c")
+    half = pl.ds(pl.multiple_of((1 - core if far else core) * 256, 256), 256)
     bias = jnp.zeros((8, 512), F32)
     for s, source in enumerate((own_ref, got1_ref, got2_ref, got3_ref)):
         q = lax.rem(x - s + 4, 4)
-        normed = jnp.concatenate([normed_ref[block(lax.rem(zl - i + 4, 4), q), :] for i in range(4)], axis=0)
+        normed = jnp.concatenate([normed_ref[block(z, q), half] for z in range(4)], axis=0)
         masked = source[...]
         part = lax.dot_general(normed, masked, (((0,), (0,)), ((), ())), preferred_element_type=F32)
         grad_ref[...] = part if s == 0 else grad_ref[...] + part
         bias = bias + jnp.dot(jnp.ones((8, 512), BF), masked, preferred_element_type=F32)
-    near = pl.ds(pl.multiple_of(core * 256, 256), 256)
-    far = pl.ds(pl.multiple_of((1 - core) * 256, 256), 256)
-    for b in range(4):
-        cols = slice(b * 128, (b + 1) * 128)
-        mine_ref[b * 256 : (b + 1) * 256, :] = grad_ref[near, cols]
-        other_ref[b * 256 : (b + 1) * 256, :] = grad_ref[far, cols].astype(BF)
     row = lax.broadcasted_iota(jnp.int32, (8, 128), 0)
     packed = jnp.zeros((8, 128), F32)
     for b in range(4):
-        packed = packed + jnp.where(row == b, bias[:, b * 128 : (b + 1) * 128], 0.0)
+        cols = slice(b * 128, (b + 1) * 128)
+        out_ref[b * 256 : (b + 1) * 256, :] = grad_ref[:, cols].astype(out_ref.dtype)
+        packed = packed + jnp.where(row == b, bias[:, cols], 0.0)
     tail = jnp.concatenate([packed, jnp.zeros((HALF - 1032, 128), F32)], axis=0)
-    mine_ref[1024:, :] = tail
-    other_ref[1024:, :] = tail.astype(BF)
+    out_ref[1024:, :] = tail.astype(out_ref.dtype)
 
 
 def piece_kernel(got_ref, out_ref):
@@ -184,12 +183,13 @@
         bias_ref[:, b * 128 : (b + 1) * 128] = jnp.sum(jnp.where(row == b, tail, 0.0), axis=0, keepdims=True)
 
 
-def key_sum_kernel(own_ref, a_ref, b_ref, c_ref, out0_ref, out1_ref, out2_ref, out3_ref):
-    zl = lax.axis_index("zl")
+def key_sum_kernel(normed_ref, weight_ref, a_ref, b_ref, c_ref, out0_ref, out1_ref, out2_ref, out3_ref):
+    x, zl = lax.axis_index("x"), lax.axis_index("zl")
     for s, out_ref in enumerate((out0_ref, out1_ref, out2_ref, out3_ref)):
-        rows = pl.ds(pl.multiple_of(lax.rem(zl + s, 4) * 128, 128), 128)
-        total = own_ref[rows, :] + a_ref[rows, :].astype(F32)
-        total = total + b_ref[rows, :].astype(F32) + c_ref[rows, :].astype(F32)
+        z = lax.rem(zl + s, 4)
+        rows = pl.ds(pl.multiple_of(z * 128, 128), 128)
+        total = jnp.dot(normed_ref[block(z, x), :], weight_ref[...], preferred_element_type=F32)
+        total = total + a_ref[rows, :].astype(F32) + b_ref[rows, :].astype(F32) + c_ref[rows, :].astype(F32)
         out_ref[...] = total.astype(out_ref.dtype)
 
 
@@ -206,30 +206,36 @@
 
 def on_device(text, image, offsets, counts, lengths, gain, weight, key_bias, cot):
     gain = gain.reshape(1, 512)
-    own = call(mask_kernel, shape((128, 512), BF), (lengths, cot), smem=1, flops=10**6, nbytes=3 * 10**5)
-    column = [own] + [shift(own, "zl", s) for s in (1, 2, 3)]
+    own = call(mask_kernel, shape((4, 128, 512), BF), (lengths, cot), smem=1, flops=10**6, nbytes=10**6)
+    column = lax.all_to_all(own, "zl", 0, 0, tiled=True).reshape(512, 512)
     split = call(prep_kernel, shape((16, 72, 512), BF), (text, image), flops=10**7, nbytes=5 * 10**6)
     images = lax.all_to_all(split, TP, 0, 0, tiled=True)
-    column = jnp.concatenate(column, axis=0)
     got = [shift(column, "x", s) for s in (1, 2, 3)]
-    normed, key0, *keys = call(
+    normed, *keys = call(
         norm_kernel,
-        [shape((2048, 512), BF), shape((512, 512), F32)] + [shape((512, 512), BF)] * 3,
+        [shape((2048, 512), BF)] + [shape((512, 512), BF)] * 3,
         (offsets, counts, text, images, weight, gain),
         smem=2,
         flops=3 * 10**9,
         nbytes=8 * 10**6,
     )
-    keys = [shift(k, "x", s + 1) for s, k in enumerate(keys)]
-    mine, other = call(
-        grad_kernel,
-        [shape((HALF, 128), F32), shape((HALF, 128), BF)],
-        (normed, column, *got),
-        scratch=[pltpu.VMEM((512, 512), F32)],
-        flops=10**9,
-        nbytes=5 * 10**6,
-    )
+    ring = []
+    for s, k in enumerate(keys):
+        ring.append(shift(k, "x", s + 1))
+
+    def grads(far, dtype):
+        return call(
+            functools.partial(grad_kernel, far),
+            shape((HALF, 128), dtype),
+            (normed, column, *got),
+            scratch=[pltpu.VMEM((256, 512), F32)],
+            flops=5 * 10**8,
+            nbytes=4 * 10**6,
+        )
+
+    other = grads(True, BF)
     far = shift(other, "c", 1)
+    mine = grads(False, F32)
     pieces = (mine + far.astype(F32)).astype(BF).reshape(PIECES, SLAB, 128)
     pieces = lax.all_to_all(pieces, RING, 0, 0, tiled=True)
     copies = call(piece_kernel, shape((PIECES, SLAB, 128), BF), (pieces,), flops=10**6, nbytes=10**6)
@@ -237,11 +243,13 @@
     sums = call(
         key_sum_kernel,
         [shape((128, 512), F32)] + [shape((128, 512), BF)] * 3,
-        (key0, *keys),
+        (normed, weight, *ring),
         flops=10**6,
         nbytes=4 * 10**6,
     )
-    parts = [shift(k, "zl", s + 1) for s, k in enumerate(sums[1:])]
+    parts = []
+    for s, k in enumerate(sums[1:]):
+        parts.append(shift(k, "zl", s + 1))
     key_states = call(
         key_kernel,
         shape((128, 512), BF),

time: 183 us -> 171 us (0.934)
  waiting for transfers between devices: 65.7 us -> 48 us
  Pallas kernels: 13.8 us -> 22 us
  starting transfers between devices: 61.8 us -> 67.1 us
  blocking collectives: 33.8 us -> 29.1 us
  local copies, waits for them, and re-layouts: 3.84 us -> 1.68 us
    ppermute x14 -> x11, waiting for transfers between devices: 59.5 us -> 27.1 us  [shift(): return lax.ppermute(value, axis, [(i, (i + by) % n) for i in range(n)])]
    all_to_all x1, waiting for transfers between devices: 0.01 us -> 13.9 us  [on_device(): images = lax.all_to_all(split, TP, 0, 0, tiled=True)]
    pallas_call x8 -> x9, Pallas kernels: 13.8 us -> 22 us  [call(): pl.pallas_call(kernel, out_shape=outs, in_specs=in_specs, out_specs=[vmem...]
    all_to_all x0 -> x1, starting transfers between devices: none -> 7.8 us  [on_device(): column = lax.all_to_all(own, 'zl', 0, 0, tiled=True).reshape(512, 512)]
    all_to_all x0 -> x1, waiting for transfers between devices: none -> 5.25 us  [on_device(): column = lax.all_to_all(own, 'zl', 0, 0, tiled=True).reshape(512, 512)]
    all_to_all x1, blocking collectives: 33.8 us -> 29.1 us  [on_device(): pieces = lax.all_to_all(pieces, RING, 0, 0, tiled=True)]
    all_to_all x1, waiting for transfers between devices: 6.17 us -> 1.72 us  [on_device(): half = lax.all_to_all(copies, RING, 0, 0, tiled=True).reshape(HALF, 128)]
    unnamed x30 -> x20, local copies, waits for them, and re-layouts: 3.83 us -> 1.67 us
  transfers between devices with their start and end apart: 16 -> 14, of which waited for: 9 -> 9; matrix products, arithmetic and copies ran while one was open for 0% -> 0% of each run, Pallas kernels for 4% -> 9%
where the time goes in v2:
time: 171 us; the launch traced here: 169 us
  starting transfers between devices  67.1 us (39%)
  waiting for transfers between devices  48 us (28%)
  blocking collectives  29.1 us (17%)
  Pallas kernels  22 us (13%)
    ppermute x11, starting transfers between devices, shift(): return lax.ppermute(value, axis, [(i, (i + by) % n) for i in range(n)])  43.4 us
    all_to_all x1, blocking collectives, on_device(): pieces = lax.all_to_all(pieces, RING, 0, 0, tiled=True)  29.1 us
    ppermute x11, waiting for transfers between devices, shift(): return lax.ppermute(value, axis, [(i, (i + by) % n) for i in range(n)])  27.1 us
    pallas_call x9, Pallas kernels, call(): pl.pallas_call(kernel, out_shape=outs, in_specs=in_specs, out_specs=[vmem...  22 us
    all_to_all x1, waiting for transfers between devices, on_device(): images = lax.all_to_all(split, TP, 0, 0, tiled=True)  13.9 us
    all_to_all x1, starting transfers between devices, on_device(): images = lax.all_to_all(split, TP, 0, 0, tiled=True)  9.28 us
    all_to_all x1, starting transfers between devices, on_device(): column = lax.all_to_all(own, 'zl', 0, 0, tiled=True).reshape(512, 512)  7.8 us
    all_to_all x1, starting transfers between devices, on_device(): half = lax.all_to_all(copies, RING, 0, 0, tiled=True).reshape(HALF, 128)  6.58 us
  transfers between devices with their start and end apart: 14, of which 9 were waited for; matrix products, arithmetic and copies ran while one was open for 0% of the time, Pallas kernels for 9%

profile of v2, /device:TPU:1, one launch (start us, length us, event | category | flops | bytes accessed | tf_op | source)
XLA Modules:
  0.0 168.8 jit_solution(5122132781977809475)
XLA Ops:
  0.6 0.0 copy-start.1
  0.6 0.0 copy-start.2
  0.7 1.0 copy-done.2
  1.6 0.7 copy-done.3
  2.3 1.4 shard_map.124
  3.7 7.8 %all-to-all-start.1 = ((bf16[4,128,512]{2,1,0:T(8,128)(2,1)}), bf16[4,128,512]{2,1,0:T(8,128)(2,1)S(1)}, u32[]{:S(2)}, u32[]{:S(2)}) async-start(bf16[4,128,512]{2,1,0:T(8,128)(2,1)} %shard_map.124), calls=%async_computation.1 | async-start | bytes 1048576 | tf_op jit(solution)/shard_map/all_to_all | solution.py:210
  11.5 0.0 copy-done.1
  11.5 3.9 %shard_map.120 = bf16[16,72,512]{2,1,0:T(8,128)(2,1)} custom-call(bf16[2048,512]{1,0:T(8,128)(2,1)} %text_ref.3, bf16[64,8192]{1,0:T(8,128)(2,1)S(1)} %copy-done.1), custom_call_target="tpu_custom_call" | custom-call | flops 10000000 | bytes 5000000 | tf_op jit(solution)/shard_map/pallas_call | solution.py:33
  15.4 5.3 %all-to-all-done.1 = bf16[4,128,512]{2,1,0:T(8,128)(2,1)S(1)} async-done(((bf16[4,128,512]{2,1,0:T(8,128)(2,1)}), bf16[4,128,512]{2,1,0:T(8,128)(2,1)S(1)}, u32[]{:S(2)}, u32[]{:S(2)}) %all-to-all-start.1) | async-done | bytes 524320 | tf_op jit(solution)/shard_map/all_to_all | solution.py:210
  20.6 9.3 %all-to-all-start = ((bf16[16,72,512]{2,1,0:T(8,128)(2,1)}), bf16[16,72,512]{2,1,0:T(8,128)(2,1)}, u32[]{:S(2)}, u32[]{:S(2)}) async-start(bf16[16,72,512]{2,1,0:T(8,128)(2,1)} %shard_map.120), calls=%async_computation | async-start | bytes 2359296 | tf_op jit(solution)/shard_map/all_to_all | solution.py:212
  29.9 3.2 %collective-permute-start.6 = (bf16[512,512]{1,0:T(8,128)(2,1)S(1)}, bf16[512,512]{1,0:T(8,128)(2,1)S(1)}, u32[]{:S(2)}, u32[]{:S(2)}) collective-permute-start(bf16[512,512]{1,0:T(8,128)(2,1)S(1)} %bitcast.5), channel_id=1, source_target_pairs={{0,1},{1,2},{2,3},{3,0},{4,5},{5,6},{6,7},{7,4},{8,9},{9,10},{10,1... | collective-permute-start | bytes 1572872 | tf_op jit(solution)/shard_map/ppermute | solution.py:204
  33.1 4.3 %collective-permute-start.7 = (bf16[512,512]{1,0:T(8,128)(2,1)S(1)}, bf16[512,512]{1,0:T(8,128)(2,1)S(1)}, u32[]{:S(2)}, u32[]{:S(2)}) collective-permute-start(bf16[512,512]{1,0:T(8,128)(2,1)S(1)} %bitcast.6), channel_id=1, source_target_pairs={{0,2},{1,3},{2,0},{3,1},{4,6},{5,7},{6,4},{7,5},{8,10},{9,11},{10,... | collective-permute-start | bytes 1572872 | tf_op jit(solution)/shard_map/ppermute | solution.py:204
  37.4 3.1 %collective-permute-start.8 = (bf16[512,512]{1,0:T(8,128)(2,1)S(1)}, bf16[512,512]{1,0:T(8,128)(2,1)S(1)}, u32[]{:S(2)}, u32[]{:S(2)}) collective-permute-start(bf16[512,512]{1,0:T(8,128)(2,1)S(1)} %bitcast.7), channel_id=1, source_target_pairs={{0,3},{1,0},{2,1},{3,2},{4,7},{5,4},{6,5},{7,6},{8,11},{9,8},{10,9... | collective-permute-start | bytes 1572872 | tf_op jit(solution)/shard_map/ppermute | solution.py:204
  40.5 0.0 copy-done.8
  40.6 13.9 %all-to-all-done.got_ref = bf16[16,72,512]{2,1,0:T(8,128)(2,1)} async-done(((bf16[16,72,512]{2,1,0:T(8,128)(2,1)}), bf16[16,72,512]{2,1,0:T(8,128)(2,1)}, u32[]{:S(2)}, u32[]{:S(2)}) %all-to-all-start) | async-done | bytes 1179680 | tf_op jit(solution)/shard_map/all_to_all | solution.py:212
  54.4 0.0 copy-done
  54.4 0.0 copy-done.6
  54.4 0.0 copy-done.7
  54.4 6.0 %shard_map.121 = (bf16[2048,512]{1,0:T(8,128)(2,1)}, bf16[512,512]{1,0:T(8,128)(2,1)}, bf16[512,512]{1,0:T(8,128)(2,1)S(1)}, bf16[512,512]{1,0:T(8,128)(2,1)S(1)}) custom-call(s32[2,2]{1,0:T(2,128)S(1)} %copy-done.6, s32[2]{0:T(128)S(1)} %copy-done.7, bf16[2048,512]{1,0:T(8,128)(2,1)} %text_ref.3, bf16[16,72,512]{2,1,0:T(8,128)(2,1)} %all-to-all-done.got_ref, ...), custom_call_target="tpu_custom_call" | custom-call | flops 3000000000 | bytes 8000000 | tf_op jit(solution)/shard_map/pallas_call | solution.py:33
  60.5 0.0 collective-permute-done.6.got1_ref
  60.5 7.6 %collective-permute-done.7.got2_ref = bf16[512,512]{1,0:T(8,128)(2,1)S(1)} collective-permute-done((bf16[512,512]{1,0:T(8,128)(2,1)S(1)}, bf16[512,512]{1,0:T(8,128)(2,1)S(1)}, u32[]{:S(2)}, u32[]{:S(2)}) %collective-permute-start.7) | collective-permute-done | bytes 524320 | tf_op jit(solution)/shard_map/ppermute | solution.py:204
  68.0 0.2 collective-permute-done.8.got3_ref
  68.2 2.6 %shard_map.126 = bf16[1152,128]{1,0:T(8,128)(2,1)S(1)} custom-call(bf16[2048,512]{1,0:T(8,128)(2,1)} %get-tuple-element.15.normed_ref, bf16[512,512]{1,0:T(8,128)(2,1)S(1)} %bitcast.8, bf16[512,512]{1,0:T(8,128)(2,1)S(1)} %collective-permute-done.6.got1_ref, bf16[512,512]{1,0:T(8,128)(2,1)S(1)} %collective-permute-done.7.got2_ref, ...), custom_call_target="tpu_custom_call" | custom-call | flops 500000000 | bytes 4000000 | tf_op jit(solution)/shard_map/pallas_call | solution.py:33
  70.8 3.6 %collective-permute-start.9 = (bf16[1152,128]{1,0:T(8,128)(2,1)S(1)}, bf16[1152,128]{1,0:T(8,128)(2,1)S(1)}, u32[]{:S(2)}, u32[]{:S(2)}) collective-permute-start(bf16[1152,128]{1,0:T(8,128)(2,1)S(1)} %shard_map.126), channel_id=1, source_target_pairs={{0,16},{16,0},{1,17},{17,1},{2,18},{18,2},{3,19},{19,3},{4,20},{20... | collective-permute-start | bytes 884744 | tf_op jit(solution)/shard_map/ppermute | solution.py:204
  74.4 2.6 %shard_map.125 = f32[1152,128]{1,0:T(8,128)S(1)} custom-call(bf16[2048,512]{1,0:T(8,128)(2,1)} %get-tuple-element.15.normed_ref, bf16[512,512]{1,0:T(8,128)(2,1)S(1)} %bitcast.9, bf16[512,512]{1,0:T(8,128)(2,1)S(1)} %collective-permute-done.6.got1_ref, bf16[512,512]{1,0:T(8,128)(2,1)S(1)} %collective-permute-done.7.got2_ref, ...), custom_call_target="tpu_custom_call" | custom-call | flops 500000000 | bytes 4000000 | tf_op jit(solution)/shard_map/pallas_call | solution.py:33
  77.1 0.0 collective-permute-done.9
  77.1 0.1 add_convert_fusion
  77.1 29.1 %all_to_all.20.got_ref = bf16[24,48,128]{2,1,0:T(8,128)(2,1)S(1)} all-to-all(bf16[24,48,128]{2,1,0:T(8,128)(2,1)S(1)} %bitcast.12), channel_id=1, replica_groups=mesh['zh'=3,'y'=8,'c'=2,'zl'=4,'x'=4] {'zh','y'}, dimensions={0} | all-to-all | bytes 589824 | tf_op jit(solution)/shard_map/all_to_all | solution.py:240
  106.3 0.8 shard_map.127
  107.1 6.6 %all-to-all-start.3 = ((bf16[24,48,128]{2,1,0:T(8,128)(2,1)}), bf16[24,48,128]{2,1,0:T(8,128)(2,1)S(1)}, u32[]{:S(2)}, u32[]{:S(2)}) async-start(bf16[24,48,128]{2,1,0:T(8,128)(2,1)} %shard_map.127), calls=%async_computation.3 | async-start | bytes 589824 | tf_op jit(solution)/shard_map/all_to_all | solution.py:242
  113.7 1.9 %collective-permute-start = (bf16[512,512]{1,0:T(8,128)(2,1)}, bf16[512,512]{1,0:T(8,128)(2,1)S(1)}, u32[]{:S(2)}, u32[]{:S(2)}) collective-permute-start(bf16[512,512]{1,0:T(8,128)(2,1)} %get-tuple-element.16), channel_id=1, source_target_pairs={{0,1},{1,2},{2,3},{3,0},{4,5},{5,6},{6,7},{7,4},{8,9},{9,10},{10,1... | collective-permute-start | bytes 1572872 | tf_op jit(solution)/shard_map/ppermute | solution.py:204
  115.6 6.7 %collective-permute-start.1 = (bf16[512,512]{1,0:T(8,128)(2,1)}, bf16[512,512]{1,0:T(8,128)(2,1)S(1)}, u32[]{:S(2)}, u32[]{:S(2)}) collective-permute-start(bf16[512,512]{1,0:T(8,128)(2,1)} %copy-done.5), channel_id=1, source_target_pairs={{0,2},{1,3},{2,0},{3,1},{4,6},{5,7},{6,4},{7,5},{8,10},{9,11},{10,... | collective-permute-start | bytes 1572872 | tf_op jit(solution)/shard_map/ppermute | solution.py:204
  122.3 1.9 %collective-permute-start.2 = (bf16[512,512]{1,0:T(8,128)(2,1)S(1)}, bf16[512,512]{1,0:T(8,128)(2,1)S(1)}, u32[]{:S(2)}, u32[]{:S(2)}) collective-permute-start(bf16[512,512]{1,0:T(8,128)(2,1)S(1)} %get-tuple-element.18), channel_id=1, source_target_pairs={{0,3},{1,0},{2,1},{3,2},{4,7},{5,4},{6,5},{7,6},{8,11},{9,8},{10,9... | collective-permute-start | bytes 1572872 | tf_op jit(solution)/shard_map/ppermute | solution.py:204
  124.2 1.7 %all-to-all-done.3 = bf16[24,48,128]{2,1,0:T(8,128)(2,1)S(1)} async-done(((bf16[24,48,128]{2,1,0:T(8,128)(2,1)}), bf16[24,48,128]{2,1,0:T(8,128)(2,1)S(1)}, u32[]{:S(2)}, u32[]{:S(2)}) %all-to-all-start.3) | async-done | bytes 294944 | tf_op jit(solution)/shard_map/all_to_all | solution.py:242
  125.9 6.5 %collective-permute-start.10 = (bf16[1152,128]{1,0:T(8,128)(2,1)S(1)}, bf16[1152,128]{1,0:T(8,128)(2,1)S(1)}, u32[]{:S(2)}, u32[]{:S(2)}) collective-permute-start(bf16[1152,128]{1,0:T(8,128)(2,1)S(1)} %bitcast.10), channel_id=1, source_target_pairs={{0,16},{16,0},{1,17},{17,1},{2,18},{18,2},{3,19},{19,3},{4,20},{20... | collective-permute-start | bytes 884744 | tf_op jit(solution)/shard_map/ppermute | solution.py:204
  132.4 0.0 collective-permute-done.a_ref
  132.5 8.0 %collective-permute-done.1.b_ref = bf16[512,512]{1,0:T(8,128)(2,1)S(1)} collective-permute-done((bf16[512,512]{1,0:T(8,128)(2,1)}, bf16[512,512]{1,0:T(8,128)(2,1)S(1)}, u32[]{:S(2)}, u32[]{:S(2)}) %collective-permute-start.1) | collective-permute-done | bytes 524320 | tf_op jit(solution)/shard_map/ppermute | solution.py:204
  140.4 4.0 %collective-permute-done.2.c_ref = bf16[512,512]{1,0:T(8,128)(2,1)S(1)} collective-permute-done((bf16[512,512]{1,0:T(8,128)(2,1)S(1)}, bf16[512,512]{1,0:T(8,128)(2,1)S(1)}, u32[]{:S(2)}, u32[]{:S(2)}) %collective-permute-start.2) | collective-permute-done | bytes 524320 | tf_op jit(solution)/shard_map/ppermute | solution.py:204
  144.4 2.1 %shard_map.122 = (f32[128,512]{1,0:T(8,128)S(1)}, bf16[128,512]{1,0:T(8,128)(2,1)S(1)}, bf16[128,512]{1,0:T(8,128)(2,1)S(1)}, bf16[128,512]{1,0:T(8,128)(2,1)S(1)}) custom-call(bf16[2048,512]{1,0:T(8,128)(2,1)} %get-tuple-element.15.normed_ref, bf16[512,512]{1,0:T(8,128)(2,1)S(1)} %copy-done, bf16[512,512]{1,0:T(8,128)(2,1)S(1)} %collective-permute-done.a_ref, ...), custom_call_target="tpu_custom_call" | custom-call | flops 1000000 | bytes 4000000 | tf_op jit(solution)/shard_map/pallas_call | solution.py:33
  146.6 5.4 %collective-permute-start.3 = (bf16[128,512]{1,0:T(8,128)(2,1)S(1)}, bf16[128,512]{1,0:T(8,128)(2,1)S(1)}, u32[]{:S(2)}, u32[]{:S(2)}) collective-permute-start(bf16[128,512]{1,0:T(8,128)(2,1)S(1)} %get-tuple-element.20), channel_id=1, source_target_pairs={{0,4},{4,8},{8,12},{12,0},{1,5},{5,9},{9,13},{13,1},{2,6},{6,10},{... | collective-permute-start | bytes 393224 | tf_op jit(solution)/shard_map/ppermute | solution.py:204
  152.0 4.9 %collective-permute-start.4 = (bf16[128,512]{1,0:T(8,128)(2,1)S(1)}, bf16[128,512]{1,0:T(8,128)(2,1)S(1)}, u32[]{:S(2)}, u32[]{:S(2)}) collective-permute-start(bf16[128,512]{1,0:T(8,128)(2,1)S(1)} %get-tuple-element.21), channel_id=1, source_target_pairs={{0,8},{4,12},{8,0},{12,4},{1,9},{5,13},{9,1},{13,5},{2,10},{6,14},... | collective-permute-start | bytes 393224 | tf_op jit(solution)/shard_map/ppermute | solution.py:204
  156.8 1.9 %collective-permute-start.5 = (bf16[128,512]{1,0:T(8,128)(2,1)S(1)}, bf16[128,512]{1,0:T(8,128)(2,1)S(1)}, u32[]{:S(2)}, u32[]{:S(2)}) collective-permute-start(bf16[128,512]{1,0:T(8,128)(2,1)S(1)} %get-tuple-element.22), channel_id=1, source_target_pairs={{0,12},{4,0},{8,4},{12,8},{1,13},{5,1},{9,5},{13,9},{2,14},{6,2},{... | collective-permute-start | bytes 393224 | tf_op jit(solution)/shard_map/ppermute | solution.py:204
  158.8 0.0 collective-permute-done.3.a_ref
  158.8 5.8 %collective-permute-done.4.b_ref = bf16[128,512]{1,0:T(8,128)(2,1)S(1)} collective-permute-done((bf16[128,512]{1,0:T(8,128)(2,1)S(1)}, bf16[128,512]{1,0:T(8,128)(2,1)S(1)}, u32[]{:S(2)}, u32[]{:S(2)}) %collective-permute-start.4) | collective-permute-done | bytes 131104 | tf_op jit(solution)/shard_map/ppermute | solution.py:204
  164.6 1.7 collective-permute-done.5.c_ref
  166.2 1.3 shard_map.123
  167.5 0.0 collective-permute-done.10.other_ref
  167.5 1.2 shard_map.128
  (13 shorter events, 0.0 us)
Async XLA Ops:
  0.6 10.8 %copy-start.1 = (bf16[64,8192]{1,0:T(8,128)(2,1)S(1)}, bf16[64,8192]{1,0:T(8,128)(2,1)}, u32[]{:S(2)}) copy-start(bf16[64,8192]{1,0:T(8,128)(2,1)} %image_ref.1) | copy-start | bytes 3145732
  0.6 1.0 copy-start.2
  1.6 0.7 copy-start.3
  3.7 16.9 %all-to-all-start.1 = ((bf16[4,128,512]{2,1,0:T(8,128)(2,1)}), bf16[4,128,512]{2,1,0:T(8,128)(2,1)S(1)}, u32[]{:S(2)}, u32[]{:S(2)}) async-start(bf16[4,128,512]{2,1,0:T(8,128)(2,1)} %shard_map.124), calls=%async_computation.1 | async-start | bytes 1048576 | tf_op jit(solution)/shard_map/all_to_all | solution.py:210
  15.3 25.2 %copy-start.8 = (bf16[512]{0:T(512)(128)(2,1)S(1)}, bf16[512]{0:T(512)(128)(2,1)}, u32[]{:S(2)}) copy-start(bf16[512]{0:T(512)(128)(2,1)} %param.14) | copy-start | bytes 3076
  15.3 39.1 %copy-start = (bf16[512,512]{1,0:T(8,128)(2,1)S(1)}, bf16[512,512]{1,0:T(8,128)(2,1)}, u32[]{:S(2)}) copy-start(bf16[512,512]{1,0:T(8,128)(2,1)} %weight_ref.5) | copy-start | bytes 1572868
  15.4 39.1 %copy-start.6 = (s32[2,2]{1,0:T(2,128)S(1)}, s32[2,2]{1,0:T(2,128)}, u32[]{:S(2)}) copy-start(s32[2,2]{1,0:T(2,128)} %offset_ref.1) | copy-start | bytes 52
  15.4 39.1 %copy-start.7 = (s32[2]{0:T(128)S(1)}, s32[2]{0:T(128)}, u32[]{:S(2)}) copy-start(s32[2]{0:T(128)} %count_ref.1) | copy-start | bytes 28
  20.6 33.8 %all-to-all-start = ((bf16[16,72,512]{2,1,0:T(8,128)(2,1)}), bf16[16,72,512]{2,1,0:T(8,128)(2,1)}, u32[]{:S(2)}, u32[]{:S(2)}) async-start(bf16[16,72,512]{2,1,0:T(8,128)(2,1)} %shard_map.120), calls=%async_computation | async-start | bytes 2359296 | tf_op jit(solution)/shard_map/all_to_all | solution.py:212
  29.9 30.6 %collective-permute-start.6 = (bf16[512,512]{1,0:T(8,128)(2,1)S(1)}, bf16[512,512]{1,0:T(8,128)(2,1)S(1)}, u32[]{:S(2)}, u32[]{:S(2)}) collective-permute-start(bf16[512,512]{1,0:T(8,128)(2,1)S(1)} %bitcast.5), channel_id=1, source_target_pairs={{0,1},{1,2},{2,3},{3,0},{4,5},{5,6},{6,7},{7,4},{8,9},{9,10},{10,1... | collective-permute-start | bytes 1572872 | tf_op jit(solution)/shard_map/ppermute | solution.py:204
  33.1 34.9 %collective-permute-start.7 = (bf16[512,512]{1,0:T(8,128)(2,1)S(1)}, bf16[512,512]{1,0:T(8,128)(2,1)S(1)}, u32[]{:S(2)}, u32[]{:S(2)}) collective-permute-start(bf16[512,512]{1,0:T(8,128)(2,1)S(1)} %bitcast.6), channel_id=1, source_target_pairs={{0,2},{1,3},{2,0},{3,1},{4,6},{5,7},{6,4},{7,5},{8,10},{9,11},{10,... | collective-permute-start | bytes 1572872 | tf_op jit(solution)/shard_map/ppermute | solution.py:204
  37.4 30.8 %collective-permute-start.8 = (bf16[512,512]{1,0:T(8,128)(2,1)S(1)}, bf16[512,512]{1,0:T(8,128)(2,1)S(1)}, u32[]{:S(2)}, u32[]{:S(2)}) collective-permute-start(bf16[512,512]{1,0:T(8,128)(2,1)S(1)} %bitcast.7), channel_id=1, source_target_pairs={{0,3},{1,0},{2,1},{3,2},{4,7},{5,4},{6,5},{7,6},{8,11},{9,8},{10,9... | collective-permute-start | bytes 1572872 | tf_op jit(solution)/shard_map/ppermute | solution.py:204
  60.5 16.7 %copy-start.5 = (bf16[512,512]{1,0:T(8,128)(2,1)}, bf16[512,512]{1,0:T(8,128)(2,1)S(1)}, u32[]{:S(2)}) copy-start(bf16[512,512]{1,0:T(8,128)(2,1)S(1)} %get-tuple-element.17) | copy-start | bytes 1572868
  70.8 6.2 %collective-permute-start.9 = (bf16[1152,128]{1,0:T(8,128)(2,1)S(1)}, bf16[1152,128]{1,0:T(8,128)(2,1)S(1)}, u32[]{:S(2)}, u32[]{:S(2)}) collective-permute-start(bf16[1152,128]{1,0:T(8,128)(2,1)S(1)} %shard_map.126), channel_id=1, source_target_pairs={{0,16},{16,0},{1,17},{17,1},{2,18},{18,2},{3,19},{19,3},{4,20},{20... | collective-permute-start | bytes 884744 | tf_op jit(solution)/shard_map/ppermute | solution.py:204
  107.1 18.8 %all-to-all-start.3 = ((bf16[24,48,128]{2,1,0:T(8,128)(2,1)}), bf16[24,48,128]{2,1,0:T(8,128)(2,1)S(1)}, u32[]{:S(2)}, u32[]{:S(2)}) async-start(bf16[24,48,128]{2,1,0:T(8,128)(2,1)} %shard_map.127), calls=%async_computation.3 | async-start | bytes 589824 | tf_op jit(solution)/shard_map/all_to_all | solution.py:242
  113.7 18.8 %collective-permute-start = (bf16[512,512]{1,0:T(8,128)(2,1)}, bf16[512,512]{1,0:T(8,128)(2,1)S(1)}, u32[]{:S(2)}, u32[]{:S(2)}) collective-permute-start(bf16[512,512]{1,0:T(8,128)(2,1)} %get-tuple-element.16), channel_id=1, source_target_pairs={{0,1},{1,2},{2,3},{3,0},{4,5},{5,6},{6,7},{7,4},{8,9},{9,10},{10,1... | collective-permute-start | bytes 1572872 | tf_op jit(solution)/shard_map/ppermute | solution.py:204
  115.6 24.8 %collective-permute-start.1 = (bf16[512,512]{1,0:T(8,128)(2,1)}, bf16[512,512]{1,0:T(8,128)(2,1)S(1)}, u32[]{:S(2)}, u32[]{:S(2)}) collective-permute-start(bf16[512,512]{1,0:T(8,128)(2,1)} %copy-done.5), channel_id=1, source_target_pairs={{0,2},{1,3},{2,0},{3,1},{4,6},{5,7},{6,4},{7,5},{8,10},{9,11},{10,... | collective-permute-start | bytes 1572872 | tf_op jit(solution)/shard_map/ppermute | solution.py:204
  122.3 22.2 %collective-permute-start.2 = (bf16[512,512]{1,0:T(8,128)(2,1)S(1)}, bf16[512,512]{1,0:T(8,128)(2,1)S(1)}, u32[]{:S(2)}, u32[]{:S(2)}) collective-permute-start(bf16[512,512]{1,0:T(8,128)(2,1)S(1)} %get-tuple-element.18), channel_id=1, source_target_pairs={{0,3},{1,0},{2,1},{3,2},{4,7},{5,4},{6,5},{7,6},{8,11},{9,8},{10,9... | collective-permute-start | bytes 1572872 | tf_op jit(solution)/shard_map/ppermute | solution.py:204
  125.9 32.9 %copy-start.9 = (bf16[512]{0:T(512)(128)(2,1)S(1)}, bf16[512]{0:T(512)(128)(2,1)}, u32[]{:S(2)}) copy-start(bf16[512]{0:T(512)(128)(2,1)} %param.16) | copy-start | bytes 3076
  125.9 40.3 %copy-start.4 = (s32[2]{0:T(128)S(1)}, s32[2]{0:T(128)}, u32[]{:S(2)}) copy-start(s32[2]{0:T(128)} %length_ref.3) | copy-start | bytes 28
  125.9 41.6 %collective-permute-start.10 = (bf16[1152,128]{1,0:T(8,128)(2,1)S(1)}, bf16[1152,128]{1,0:T(8,128)(2,1)S(1)}, u32[]{:S(2)}, u32[]{:S(2)}) collective-permute-start(bf16[1152,128]{1,0:T(8,128)(2,1)S(1)} %bitcast.10), channel_id=1, source_target_pairs={{0,16},{16,0},{1,17},{17,1},{2,18},{18,2},{3,19},{19,3},{4,20},{20... | collective-permute-start | bytes 884744 | tf_op jit(solution)/shard_map/ppermute | solution.py:204
  146.6 12.2 %collective-permute-start.3 = (bf16[128,512]{1,0:T(8,128)(2,1)S(1)}, bf16[128,512]{1,0:T(8,128)(2,1)S(1)}, u32[]{:S(2)}, u32[]{:S(2)}) collective-permute-start(bf16[128,512]{1,0:T(8,128)(2,1)S(1)} %get-tuple-element.20), channel_id=1, source_target_pairs={{0,4},{4,8},{8,12},{12,0},{1,5},{5,9},{9,13},{13,1},{2,6},{6,10},{... | collective-permute-start | bytes 393224 | tf_op jit(solution)/shard_map/ppermute | solution.py:204
  152.0 12.6 %collective-permute-start.4 = (bf16[128,512]{1,0:T(8,128)(2,1)S(1)}, bf16[128,512]{1,0:T(8,128)(2,1)S(1)}, u32[]{:S(2)}, u32[]{:S(2)}) collective-permute-start(bf16[128,512]{1,0:T(8,128)(2,1)S(1)} %get-tuple-element.21), channel_id=1, source_target_pairs={{0,8},{4,12},{8,0},{12,4},{1,9},{5,13},{9,1},{13,5},{2,10},{6,14},... | collective-permute-start | bytes 393224 | tf_op jit(solution)/shard_map/ppermute | solution.py:204
  156.8 9.4 %collective-permute-start.5 = (bf16[128,512]{1,0:T(8,128)(2,1)S(1)}, bf16[128,512]{1,0:T(8,128)(2,1)S(1)}, u32[]{:S(2)}, u32[]{:S(2)}) collective-permute-start(bf16[128,512]{1,0:T(8,128)(2,1)S(1)} %get-tuple-element.22), channel_id=1, source_target_pairs={{0,12},{4,0},{8,4},{12,8},{1,13},{5,1},{9,5},{13,9},{2,14},{6,2},{... | collective-permute-start | bytes 393224 | tf_op jit(solution)/shard_map/ppermute | solution.py:204

commit v3 on v1

--- a/solution.py
+++ b/solution.py
@@ -23,7 +23,7 @@
 MIB = 1024 * 1024
 
 
-def call(kernel, outs, args, smem=0, scratch=(), flops=0, nbytes=0, mib=12):
+def call(kernel, outs, args, smem=0, scratch=(), flops=0, nbytes=0, mib=50):
     in_specs = [pl.BlockSpec(memory_space=pltpu.SMEM)] * smem
     in_specs += [pl.BlockSpec(memory_space=pltpu.VMEM)] * (len(args) - smem)
     many = isinstance(outs, (list, tuple))
@@ -86,7 +86,7 @@
 
 
 def norm_kernel(
-    offset_ref, count_ref, text_ref, got_ref, weight_ref, gain_ref, normed_ref, key0_ref, key1_ref, key2_ref, key3_ref
+    offset_ref, count_ref, text_ref, got_ref, weight_ref, gain_ref, normed_ref, key1_ref, key2_ref, key3_ref
 ):
     squares = jnp.concatenate([got_ref[t, 64:, :] for t in range(16)], axis=0)
     pick = lax.broadcasted_iota(jnp.int32, (128, 128), 0) % 4
@@ -119,11 +119,10 @@
                 value = jnp.where(covered, placed[:, cols], text) * scale * gain[:, cols]
                 normed_ref[rows, cols] = value.astype(BF)
     x = lax.axis_index("x")
-    for s, key_ref in enumerate((key0_ref, key1_ref, key2_ref, key3_ref)):
-        q = lax.rem(x + s, 4)
+    for s, key_ref in enumerate((key1_ref, key2_ref, key3_ref)):
+        q = lax.rem(x + s + 1, 4)
         normed = jnp.concatenate([normed_ref[block(z, q), :] for z in range(4)], axis=0)
-        product = jnp.dot(normed, weight_ref[...], preferred_element_type=F32)
-        key_ref[...] = product.astype(key_ref.dtype)
+        key_ref[...] = jnp.dot(normed, weight_ref[...], preferred_element_type=F32).astype(BF)
 
 
 def grad_kernel(normed_ref, own_ref, got1_ref, got2_ref, got3_ref, mine_ref, other_ref, grad_ref):
@@ -184,12 +183,13 @@
         bias_ref[:, b * 128 : (b + 1) * 128] = jnp.sum(jnp.where(row == b, tail, 0.0), axis=0, keepdims=True)
 
 
-def key_sum_kernel(own_ref, a_ref, b_ref, c_ref, out0_ref, out1_ref, out2_ref, out3_ref):
-    zl = lax.axis_index("zl")
+def key_sum_kernel(normed_ref, weight_ref, a_ref, b_ref, c_ref, out0_ref, out1_ref, out2_ref, out3_ref):
+    x, zl = lax.axis_index("x"), lax.axis_index("zl")
     for s, out_ref in enumerate((out0_ref, out1_ref, out2_ref, out3_ref)):
-        rows = pl.ds(pl.multiple_of(lax.rem(zl + s, 4) * 128, 128), 128)
-        total = own_ref[rows, :] + a_ref[rows, :].astype(F32)
-        total = total + b_ref[rows, :].astype(F32) + c_ref[rows, :].astype(F32)
+        z = lax.rem(zl + s, 4)
+        rows = pl.ds(pl.multiple_of(z * 128, 128), 128)
+        total = jnp.dot(normed_ref[block(z, x), :], weight_ref[...], preferred_element_type=F32)
+        total = total + a_ref[rows, :].astype(F32) + b_ref[rows, :].astype(F32) + c_ref[rows, :].astype(F32)
         out_ref[...] = total.astype(out_ref.dtype)
 
 
@@ -212,15 +212,18 @@
     images = lax.all_to_all(split, TP, 0, 0, tiled=True)
     column = jnp.concatenate(column, axis=0)
     got = [shift(column, "x", s) for s in (1, 2, 3)]
-    normed, key0, *keys = call(
+    normed, *keys = call(
         norm_kernel,
-        [shape((2048, 512), BF), shape((512, 512), F32)] + [shape((512, 512), BF)] * 3,
+        [shape((2048, 512), BF)] + [shape((512, 512), BF)] * 3,
         (offsets, counts, text, images, weight, gain),
         smem=2,
         flops=3 * 10**9,
         nbytes=8 * 10**6,
     )
-    keys = [shift(k, "x", s + 1) for s, k in enumerate(keys)]
+    ring = []
+    for s, k in enumerate(keys):
+        ring.append(shift(k, "x", s + 1))
+
     mine, other = call(
         grad_kernel,
         [shape((HALF, 128), F32), shape((HALF, 128), BF)],
@@ -237,11 +240,13 @@
     sums = call(
         key_sum_kernel,
         [shape((128, 512), F32)] + [shape((128, 512), BF)] * 3,
-        (key0, *keys),
+        (normed, weight, *ring),
         flops=10**6,
         nbytes=4 * 10**6,
     )
-    parts = [shift(k, "zl", s + 1) for s, k in enumerate(sums[1:])]
+    parts = []
+    for s, k in enumerate(sums[1:]):
+        parts.append(shift(k, "zl", s + 1))
     key_states = call(
         key_kernel,
         shape((128, 512), BF),

time: 183 us -> 185 us (1.011)
  Pallas kernels: 13.8 us -> 18.9 us
  local copies, waits for them, and re-layouts: 3.84 us -> 1.27 us
    pallas_call x8, Pallas kernels: 13.8 us -> 18.9 us  [call(): pl.pallas_call(kernel, out_shape=outs, in_specs=in_specs, out_specs=[vmem...]
    unnamed x30 -> x22, local copies, waits for them, and re-layouts: 3.83 us -> 1.26 us
  transfers between devices with their start and end apart: 16 -> 16, of which waited for: 9 -> 10; matrix products, arithmetic and copies ran while one was open for 0% -> 0% of each run, Pallas kernels for 4% -> 5%
where the time goes in v3:
time: 185 us; the launch traced here: 182 us
  waiting for transfers between devices  66.5 us (36%)
  starting transfers between devices  61.3 us (33%)
  blocking collectives  33 us (18%)
  Pallas kernels  18.9 us (10%)
    ppermute x14, waiting for transfers between devices, shift(): return lax.ppermute(value, axis, [(i, (i + by) % n) for i in range(n)])  60.4 us
    ppermute x14, starting transfers between devices, shift(): return lax.ppermute(value, axis, [(i, (i + by) % n) for i in range(n)])  44.9 us
    all_to_all x1, blocking collectives, on_device(): pieces = lax.all_to_all(pieces, RING, 0, 0, tiled=True)  33 us
    pallas_call x8, Pallas kernels, call(): pl.pallas_call(kernel, out_shape=outs, in_specs=in_specs, out_specs=[vmem...  18.9 us
    all_to_all x1, starting transfers between devices, on_device(): images = lax.all_to_all(split, TP, 0, 0, tiled=True)  10.5 us
    all_to_all x1, waiting for transfers between devices, on_device(): half = lax.all_to_all(copies, RING, 0, 0, tiled=True).reshape(HALF, 128)  6.17 us
    all_to_all x1, starting transfers between devices, on_device(): half = lax.all_to_all(copies, RING, 0, 0, tiled=True).reshape(HALF, 128)  5.92 us
  transfers between devices with their start and end apart: 16, of which 10 were waited for; matrix products, arithmetic and copies ran while one was open for 0% of the time, Pallas kernels for 5%

profile of v3, /device:TPU:1, one launch (start us, length us, event | category | flops | bytes accessed | tf_op | source)
XLA Modules:
  0.0 182.0 jit_solution(16177583413457447756)
XLA Ops:
  0.6 1.2 copy-done.1
  1.9 3.9 %shard_map.120 = bf16[16,72,512]{2,1,0:T(8,128)(2,1)} custom-call(bf16[2048,512]{1,0:T(8,128)(2,1)} %text_ref.3, bf16[64,8192]{1,0:T(8,128)(2,1)S(1)} %copy-done.1), custom_call_target="tpu_custom_call" | custom-call | flops 10000000 | bytes 5000000 | tf_op jit(solution)/shard_map/pallas_call | solution.py:31
  5.7 0.0 copy-start.7
  5.7 0.0 copy-start.8
  5.7 10.5 %all-to-all-start = ((bf16[16,72,512]{2,1,0:T(8,128)(2,1)}), bf16[16,72,512]{2,1,0:T(8,128)(2,1)S(1)}, u32[]{:S(2)}, u32[]{:S(2)}) async-start(bf16[16,72,512]{2,1,0:T(8,128)(2,1)} %shard_map.120), calls=%async_computation | async-start | bytes 2359296 | tf_op jit(solution)/shard_map/all_to_all | solution.py:212
  16.3 0.6 shard_map.124
  16.9 5.1 %collective-permute-start.8 = (bf16[128,512]{1,0:T(8,128)(2,1)S(1)}, bf16[128,512]{1,0:T(8,128)(2,1)S(1)}, u32[]{:S(2)}, u32[]{:S(2)}) collective-permute-start(bf16[128,512]{1,0:T(8,128)(2,1)S(1)} %shard_map.124), channel_id=1, source_target_pairs={{0,12},{4,0},{8,4},{12,8},{1,13},{5,1},{9,5},{13,9},{2,14},{6,2},{... | collective-permute-start | bytes 393224 | tf_op jit(solution)/shard_map/ppermute | solution.py:204
  22.0 1.9 %collective-permute-start.7 = (bf16[128,512]{1,0:T(8,128)(2,1)S(1)}, bf16[128,512]{1,0:T(8,128)(2,1)S(1)}, u32[]{:S(2)}, u32[]{:S(2)}) collective-permute-start(bf16[128,512]{1,0:T(8,128)(2,1)S(1)} %shard_map.124), channel_id=1, source_target_pairs={{0,8},{4,12},{8,0},{12,4},{1,9},{5,13},{9,1},{13,5},{2,10},{6,14},... | collective-permute-start | bytes 393224 | tf_op jit(solution)/shard_map/ppermute | solution.py:204
  23.9 2.5 %collective-permute-start.6 = (bf16[128,512]{1,0:T(8,128)(2,1)S(1)}, bf16[128,512]{1,0:T(8,128)(2,1)S(1)}, u32[]{:S(2)}, u32[]{:S(2)}) collective-permute-start(bf16[128,512]{1,0:T(8,128)(2,1)S(1)} %shard_map.124), channel_id=1, source_target_pairs={{0,4},{4,8},{8,12},{12,0},{1,5},{5,9},{9,13},{13,1},{2,6},{6,10},{... | collective-permute-start | bytes 393224 | tf_op jit(solution)/shard_map/ppermute | solution.py:204
  26.4 8.5 %collective-permute-done.8 = bf16[128,512]{1,0:T(8,128)(2,1)S(1)} collective-permute-done((bf16[128,512]{1,0:T(8,128)(2,1)S(1)}, bf16[128,512]{1,0:T(8,128)(2,1)S(1)}, u32[]{:S(2)}, u32[]{:S(2)}) %collective-permute-start.8) | collective-permute-done | bytes 131104 | tf_op jit(solution)/shard_map/ppermute | solution.py:204
  34.8 20.8 %collective-permute-done.7 = bf16[128,512]{1,0:T(8,128)(2,1)S(1)} collective-permute-done((bf16[128,512]{1,0:T(8,128)(2,1)S(1)}, bf16[128,512]{1,0:T(8,128)(2,1)S(1)}, u32[]{:S(2)}, u32[]{:S(2)}) %collective-permute-start.7) | collective-permute-done | bytes 131104 | tf_op jit(solution)/shard_map/ppermute | solution.py:204
  55.6 0.0 collective-permute-done.6
  55.6 3.1 %collective-permute-start.9 = (bf16[512,512]{1,0:T(8,128)(2,1)S(1)}, bf16[512,512]{1,0:T(8,128)(2,1)S(1)}, u32[]{:S(2)}, u32[]{:S(2)}) collective-permute-start(bf16[512,512]{1,0:T(8,128)(2,1)S(1)} %pad_maximum_fusion.own_ref), channel_id=1, source_target_pairs={{0,1},{1,2},{2,3},{3,0},{4,5},{5,6},{6,7},{7,4},{8,9},{9,10},{10,1... | collective-permute-start | bytes 1572872 | tf_op jit(solution)/shard_map/ppermute | solution.py:204
  58.7 3.2 %collective-permute-start.10 = (bf16[512,512]{1,0:T(8,128)(2,1)S(1)}, bf16[512,512]{1,0:T(8,128)(2,1)S(1)}, u32[]{:S(2)}, u32[]{:S(2)}) collective-permute-start(bf16[512,512]{1,0:T(8,128)(2,1)S(1)} %pad_maximum_fusion.own_ref), channel_id=1, source_target_pairs={{0,2},{1,3},{2,0},{3,1},{4,6},{5,7},{6,4},{7,5},{8,10},{9,11},{10,... | collective-permute-start | bytes 1572872 | tf_op jit(solution)/shard_map/ppermute | solution.py:204
  61.9 3.1 %collective-permute-start.11 = (bf16[512,512]{1,0:T(8,128)(2,1)S(1)}, bf16[512,512]{1,0:T(8,128)(2,1)}, u32[]{:S(2)}, u32[]{:S(2)}) collective-permute-start(bf16[512,512]{1,0:T(8,128)(2,1)S(1)} %pad_maximum_fusion.own_ref), channel_id=1, source_target_pairs={{0,3},{1,0},{2,1},{3,2},{4,7},{5,4},{6,5},{7,6},{8,11},{9,8},{10,9... | collective-permute-start | bytes 1572872 | tf_op jit(solution)/shard_map/ppermute | solution.py:204
  65.0 0.0 all-to-all-done.got_ref
  65.0 0.0 copy-done
  65.1 0.0 copy-done.7
  65.1 0.0 copy-done.8
  65.1 5.7 %shard_map.121 = (bf16[2048,512]{1,0:T(8,128)(2,1)}, bf16[512,512]{1,0:T(8,128)(2,1)}, bf16[512,512]{1,0:T(8,128)(2,1)S(1)}, bf16[512,512]{1,0:T(8,128)(2,1)S(1)}) custom-call(s32[2,2]{1,0:T(2,128)S(1)} %copy-done.7, s32[2]{0:T(128)S(1)} %copy-done.8, bf16[2048,512]{1,0:T(8,128)(2,1)} %text_ref.3, bf16[16,72,512]{2,1,0:T(8,128)(2,1)S(1)} %all-to-all-done.got_ref, ...), custom_call_target="tpu_custom_call" | custom-call | flops 3000000000 | bytes 8000000 | tf_op jit(solution)/shard_map/pallas_call | solution.py:31
  70.8 1.3 collective-permute-done.9.got1_ref
  72.1 8.7 %collective-permute-done.10.got2_ref = bf16[512,512]{1,0:T(8,128)(2,1)S(1)} collective-permute-done((bf16[512,512]{1,0:T(8,128)(2,1)S(1)}, bf16[512,512]{1,0:T(8,128)(2,1)S(1)}, u32[]{:S(2)}, u32[]{:S(2)}) %collective-permute-start.10) | collective-permute-done | bytes 524320 | tf_op jit(solution)/shard_map/ppermute | solution.py:204
  80.8 4.5 %collective-permute-done.11.got3_ref = bf16[512,512]{1,0:T(8,128)(2,1)} collective-permute-done((bf16[512,512]{1,0:T(8,128)(2,1)S(1)}, bf16[512,512]{1,0:T(8,128)(2,1)}, u32[]{:S(2)}, u32[]{:S(2)}) %collective-permute-start.11) | collective-permute-done | bytes 524320 | tf_op jit(solution)/shard_map/ppermute | solution.py:204
  85.3 3.3 %shard_map.125 = (f32[1152,128]{1,0:T(8,128)S(1)}, bf16[1152,128]{1,0:T(8,128)(2,1)S(1)}) custom-call(bf16[2048,512]{1,0:T(8,128)(2,1)} %get-tuple-element.17.normed_ref, bf16[512,512]{1,0:T(8,128)(2,1)S(1)} %pad_maximum_fusion.own_ref, bf16[512,512]{1,0:T(8,128)(2,1)S(1)} %collective-permute-done.9.got1_ref, ...), custom_call_target="tpu_custom_call" | custom-call | flops 1000000000 | bytes 5000000 | tf_op jit(solution)/shard_map/pallas_call | solution.py:31
  88.6 3.7 %collective-permute-start.12 = (bf16[1152,128]{1,0:T(8,128)(2,1)S(1)}, bf16[1152,128]{1,0:T(8,128)(2,1)S(1)}, u32[]{:S(2)}, u32[]{:S(2)}) collective-permute-start(bf16[1152,128]{1,0:T(8,128)(2,1)S(1)} %get-tuple-element.26), channel_id=1, source_target_pairs={{0,16},{16,0},{1,17},{17,1},{2,18},{18,2},{3,19},{19,3},{4,20},{20... | collective-permute-start | bytes 884744 | tf_op jit(solution)/shard_map/ppermute | solution.py:204
  92.4 1.2 collective-permute-done.12
  93.5 0.1 add_convert_fusion
  93.6 33.0 %all_to_all.15.got_ref = bf16[24,48,128]{2,1,0:T(8,128)(2,1)S(1)} all-to-all(bf16[24,48,128]{2,1,0:T(8,128)(2,1)S(1)} %bitcast.6), channel_id=1, replica_groups=mesh['zh'=3,'y'=8,'c'=2,'zl'=4,'x'=4] {'zh','y'}, dimensions={0} | all-to-all | bytes 589824 | tf_op jit(solution)/shard_map/all_to_all | solution.py:237
  126.6 0.8 shard_map.126
  127.4 5.9 %all-to-all-start.2 = ((bf16[24,48,128]{2,1,0:T(8,128)(2,1)}), bf16[24,48,128]{2,1,0:T(8,128)(2,1)S(1)}, u32[]{:S(2)}, u32[]{:S(2)}) async-start(bf16[24,48,128]{2,1,0:T(8,128)(2,1)} %shard_map.126), calls=%async_computation.2 | async-start | bytes 589824 | tf_op jit(solution)/shard_map/all_to_all | solution.py:239
  133.3 3.8 %collective-permute-start = (bf16[512,512]{1,0:T(8,128)(2,1)}, bf16[512,512]{1,0:T(8,128)(2,1)S(1)}, u32[]{:S(2)}, u32[]{:S(2)}) collective-permute-start(bf16[512,512]{1,0:T(8,128)(2,1)} %get-tuple-element.18), channel_id=1, source_target_pairs={{0,1},{1,2},{2,3},{3,0},{4,5},{5,6},{6,7},{7,4},{8,9},{9,10},{10,1... | collective-permute-start | bytes 1572872 | tf_op jit(solution)/shard_map/ppermute | solution.py:204
  137.1 3.6 %collective-permute-start.1 = (bf16[512,512]{1,0:T(8,128)(2,1)}, bf16[512,512]{1,0:T(8,128)(2,1)S(1)}, u32[]{:S(2)}, u32[]{:S(2)}) collective-permute-start(bf16[512,512]{1,0:T(8,128)(2,1)} %copy-done.6), channel_id=1, source_target_pairs={{0,2},{1,3},{2,0},{3,1},{4,6},{5,7},{6,4},{7,5},{8,10},{9,11},{10,... | collective-permute-start | bytes 1572872 | tf_op jit(solution)/shard_map/ppermute | solution.py:204
  140.7 3.0 %collective-permute-start.2 = (bf16[512,512]{1,0:T(8,128)(2,1)S(1)}, bf16[512,512]{1,0:T(8,128)(2,1)S(1)}, u32[]{:S(2)}, u32[]{:S(2)}) collective-permute-start(bf16[512,512]{1,0:T(8,128)(2,1)S(1)} %copy-done.5), channel_id=1, source_target_pairs={{0,3},{1,0},{2,1},{3,2},{4,7},{5,4},{6,5},{7,6},{8,11},{9,8},{10,9... | collective-permute-start | bytes 1572872 | tf_op jit(solution)/shard_map/ppermute | solution.py:204
  143.7 6.2 %all-to-all-done.2 = bf16[24,48,128]{2,1,0:T(8,128)(2,1)S(1)} async-done(((bf16[24,48,128]{2,1,0:T(8,128)(2,1)}), bf16[24,48,128]{2,1,0:T(8,128)(2,1)S(1)}, u32[]{:S(2)}, u32[]{:S(2)}) %all-to-all-start.2) | async-done | bytes 294944 | tf_op jit(solution)/shard_map/all_to_all | solution.py:239
  149.8 3.0 %collective-permute-start.13 = (bf16[1152,128]{1,0:T(8,128)(2,1)S(1)}, bf16[1152,128]{1,0:T(8,128)(2,1)S(1)}, u32[]{:S(2)}, u32[]{:S(2)}) collective-permute-start(bf16[1152,128]{1,0:T(8,128)(2,1)S(1)} %bitcast.4), channel_id=1, source_target_pairs={{0,16},{16,0},{1,17},{17,1},{2,18},{18,2},{3,19},{19,3},{4,20},{20... | collective-permute-start | bytes 884744 | tf_op jit(solution)/shard_map/ppermute | solution.py:204
  152.8 0.0 collective-permute-done.a_ref
  152.9 8.2 %collective-permute-done.1.b_ref = bf16[512,512]{1,0:T(8,128)(2,1)S(1)} collective-permute-done((bf16[512,512]{1,0:T(8,128)(2,1)}, bf16[512,512]{1,0:T(8,128)(2,1)S(1)}, u32[]{:S(2)}, u32[]{:S(2)}) %collective-permute-start.1) | collective-permute-done | bytes 524320 | tf_op jit(solution)/shard_map/ppermute | solution.py:204
  161.1 2.1 %collective-permute-done.2.c_ref = bf16[512,512]{1,0:T(8,128)(2,1)S(1)} collective-permute-done((bf16[512,512]{1,0:T(8,128)(2,1)S(1)}, bf16[512,512]{1,0:T(8,128)(2,1)S(1)}, u32[]{:S(2)}, u32[]{:S(2)}) %collective-permute-start.2) | collective-permute-done | bytes 524320 | tf_op jit(solution)/shard_map/ppermute | solution.py:204
  163.2 2.1 %shard_map.122 = (f32[128,512]{1,0:T(8,128)S(1)}, bf16[128,512]{1,0:T(8,128)(2,1)S(1)}, bf16[128,512]{1,0:T(8,128)(2,1)S(1)}, bf16[128,512]{1,0:T(8,128)(2,1)S(1)}) custom-call(bf16[2048,512]{1,0:T(8,128)(2,1)} %get-tuple-element.17.normed_ref, bf16[512,512]{1,0:T(8,128)(2,1)S(1)} %copy-done, bf16[512,512]{1,0:T(8,128)(2,1)S(1)} %collective-permute-done.a_ref, ...), custom_call_target="tpu_custom_call" | custom-call | flops 1000000 | bytes 4000000 | tf_op jit(solution)/shard_map/pallas_call | solution.py:31
  165.3 1.9 %collective-permute-start.3 = (bf16[128,512]{1,0:T(8,128)(2,1)S(1)}, bf16[128,512]{1,0:T(8,128)(2,1)S(1)}, u32[]{:S(2)}, u32[]{:S(2)}) collective-permute-start(bf16[128,512]{1,0:T(8,128)(2,1)S(1)} %get-tuple-element.22), channel_id=1, source_target_pairs={{0,4},{4,8},{8,12},{12,0},{1,5},{5,9},{9,13},{13,1},{2,6},{6,10},{... | collective-permute-start | bytes 393224 | tf_op jit(solution)/shard_map/ppermute | solution.py:204
  167.2 1.9 %collective-permute-start.4 = (bf16[128,512]{1,0:T(8,128)(2,1)S(1)}, bf16[128,512]{1,0:T(8,128)(2,1)S(1)}, u32[]{:S(2)}, u32[]{:S(2)}) collective-permute-start(bf16[128,512]{1,0:T(8,128)(2,1)S(1)} %get-tuple-element.23), channel_id=1, source_target_pairs={{0,8},{4,12},{8,0},{12,4},{1,9},{5,13},{9,1},{13,5},{2,10},{6,14},... | collective-permute-start | bytes 393224 | tf_op jit(solution)/shard_map/ppermute | solution.py:204
  169.1 5.2 %collective-permute-start.5 = (bf16[128,512]{1,0:T(8,128)(2,1)S(1)}, bf16[128,512]{1,0:T(8,128)(2,1)S(1)}, u32[]{:S(2)}, u32[]{:S(2)}) collective-permute-start(bf16[128,512]{1,0:T(8,128)(2,1)S(1)} %get-tuple-element.24), channel_id=1, source_target_pairs={{0,12},{4,0},{8,4},{12,8},{1,13},{5,1},{9,5},{13,9},{2,14},{6,2},{... | collective-permute-start | bytes 393224 | tf_op jit(solution)/shard_map/ppermute | solution.py:204
  174.3 0.0 collective-permute-done.3.a_ref
  174.3 5.1 %collective-permute-done.4.b_ref = bf16[128,512]{1,0:T(8,128)(2,1)S(1)} collective-permute-done((bf16[128,512]{1,0:T(8,128)(2,1)S(1)}, bf16[128,512]{1,0:T(8,128)(2,1)S(1)}, u32[]{:S(2)}, u32[]{:S(2)}) %collective-permute-start.4) | collective-permute-done | bytes 131104 | tf_op jit(solution)/shard_map/ppermute | solution.py:204
  179.5 0.0 collective-permute-done.5.c_ref
  179.5 1.3 shard_map.123
  180.8 0.0 collective-permute-done.13.other_ref
  180.8 1.2 shard_map.127
  (19 shorter events, 0.1 us)
Async XLA Ops:
  0.6 1.2 copy-start.1
  5.7 10.6 %copy-start.2 = (bf16[128,512]{1,0:T(8,128)(2,1)S(1)}, bf16[128,512]{1,0:T(8,128)(2,1)}, u32[]{:S(2)}) copy-start(bf16[128,512]{1,0:T(8,128)(2,1)} %cot_ref.1) | copy-start | bytes 393220
  5.7 10.6 %copy-start.3 = (s32[2]{0:T(128)S(1)}, s32[2]{0:T(128)}, u32[]{:S(2)}) copy-start(s32[2]{0:T(128)} %length_ref.3) | copy-start | bytes 28
  5.7 59.3 %copy-start.9 = (bf16[512]{0:T(512)(128)(2,1)S(1)}, bf16[512]{0:T(512)(128)(2,1)}, u32[]{:S(2)}) copy-start(bf16[512]{0:T(512)(128)(2,1)} %param.14) | copy-start | bytes 3076
  5.7 59.3 %copy-start = (bf16[512,512]{1,0:T(8,128)(2,1)S(1)}, bf16[512,512]{1,0:T(8,128)(2,1)}, u32[]{:S(2)}) copy-start(bf16[512,512]{1,0:T(8,128)(2,1)} %weight_ref.5) | copy-start | bytes 1572868
  5.7 59.3 %copy-start.7 = (s32[2,2]{1,0:T(2,128)S(1)}, s32[2,2]{1,0:T(2,128)}, u32[]{:S(2)}) copy-start(s32[2,2]{1,0:T(2,128)} %offset_ref.1) | copy-start | bytes 52
  5.7 59.3 %copy-start.8 = (s32[2]{0:T(128)S(1)}, s32[2]{0:T(128)}, u32[]{:S(2)}) copy-start(s32[2]{0:T(128)} %count_ref.1) | copy-start | bytes 28
  5.7 59.3 %all-to-all-start = ((bf16[16,72,512]{2,1,0:T(8,128)(2,1)}), bf16[16,72,512]{2,1,0:T(8,128)(2,1)S(1)}, u32[]{:S(2)}, u32[]{:S(2)}) async-start(bf16[16,72,512]{2,1,0:T(8,128)(2,1)} %shard_map.120), calls=%async_computation | async-start | bytes 2359296 | tf_op jit(solution)/shard_map/all_to_all | solution.py:212
  16.9 17.9 %collective-permute-start.8 = (bf16[128,512]{1,0:T(8,128)(2,1)S(1)}, bf16[128,512]{1,0:T(8,128)(2,1)S(1)}, u32[]{:S(2)}, u32[]{:S(2)}) collective-permute-start(bf16[128,512]{1,0:T(8,128)(2,1)S(1)} %shard_map.124), channel_id=1, source_target_pairs={{0,12},{4,0},{8,4},{12,8},{1,13},{5,1},{9,5},{13,9},{2,14},{6,2},{... | collective-permute-start | bytes 393224 | tf_op jit(solution)/shard_map/ppermute | solution.py:204
  22.0 33.6 %collective-permute-start.7 = (bf16[128,512]{1,0:T(8,128)(2,1)S(1)}, bf16[128,512]{1,0:T(8,128)(2,1)S(1)}, u32[]{:S(2)}, u32[]{:S(2)}) collective-permute-start(bf16[128,512]{1,0:T(8,128)(2,1)S(1)} %shard_map.124), channel_id=1, source_target_pairs={{0,8},{4,12},{8,0},{12,4},{1,9},{5,13},{9,1},{13,5},{2,10},{6,14},... | collective-permute-start | bytes 393224 | tf_op jit(solution)/shard_map/ppermute | solution.py:204
  23.9 31.7 %collective-permute-start.6 = (bf16[128,512]{1,0:T(8,128)(2,1)S(1)}, bf16[128,512]{1,0:T(8,128)(2,1)S(1)}, u32[]{:S(2)}, u32[]{:S(2)}) collective-permute-start(bf16[128,512]{1,0:T(8,128)(2,1)S(1)} %shard_map.124), channel_id=1, source_target_pairs={{0,4},{4,8},{8,12},{12,0},{1,5},{5,9},{9,13},{13,1},{2,6},{6,10},{... | collective-permute-start | bytes 393224 | tf_op jit(solution)/shard_map/ppermute | solution.py:204
  55.6 16.5 %collective-permute-start.9 = (bf16[512,512]{1,0:T(8,128)(2,1)S(1)}, bf16[512,512]{1,0:T(8,128)(2,1)S(1)}, u32[]{:S(2)}, u32[]{:S(2)}) collective-permute-start(bf16[512,512]{1,0:T(8,128)(2,1)S(1)} %pad_maximum_fusion.own_ref), channel_id=1, source_target_pairs={{0,1},{1,2},{2,3},{3,0},{4,5},{5,6},{6,7},{7,4},{8,9},{9,10},{10,1... | collective-permute-start | bytes 1572872 | tf_op jit(solution)/shard_map/ppermute | solution.py:204
  58.7 22.1 %collective-permute-start.10 = (bf16[512,512]{1,0:T(8,128)(2,1)S(1)}, bf16[512,512]{1,0:T(8,128)(2,1)S(1)}, u32[]{:S(2)}, u32[]{:S(2)}) collective-permute-start(bf16[512,512]{1,0:T(8,128)(2,1)S(1)} %pad_maximum_fusion.own_ref), channel_id=1, source_target_pairs={{0,2},{1,3},{2,0},{3,1},{4,6},{5,7},{6,4},{7,5},{8,10},{9,11},{10,... | collective-permute-start | bytes 1572872 | tf_op jit(solution)/shard_map/ppermute | solution.py:204
  61.9 23.4 %collective-permute-start.11 = (bf16[512,512]{1,0:T(8,128)(2,1)S(1)}, bf16[512,512]{1,0:T(8,128)(2,1)}, u32[]{:S(2)}, u32[]{:S(2)}) collective-permute-start(bf16[512,512]{1,0:T(8,128)(2,1)S(1)} %pad_maximum_fusion.own_ref), channel_id=1, source_target_pairs={{0,3},{1,0},{2,1},{3,2},{4,7},{5,4},{6,5},{7,6},{8,11},{9,8},{10,9... | collective-permute-start | bytes 1572872 | tf_op jit(solution)/shard_map/ppermute | solution.py:204
  70.8 17.8 %copy-start.4 = (bf16[512,512]{1,0:T(8,128)(2,1)}, bf16[512,512]{1,0:T(8,128)(2,1)S(1)}, u32[]{:S(2)}) copy-start(bf16[512,512]{1,0:T(8,128)(2,1)S(1)} %get-tuple-element.20) | copy-start | bytes 1572868
  70.8 22.8 %copy-start.6 = (bf16[512,512]{1,0:T(8,128)(2,1)}, bf16[512,512]{1,0:T(8,128)(2,1)S(1)}, u32[]{:S(2)}) copy-start(bf16[512,512]{1,0:T(8,128)(2,1)S(1)} %get-tuple-element.19) | copy-start | bytes 1572868
  88.6 52.0 %copy-start.5 = (bf16[512,512]{1,0:T(8,128)(2,1)S(1)}, bf16[512,512]{1,0:T(8,128)(2,1)}, u32[]{:S(2)}) copy-start(bf16[512,512]{1,0:T(8,128)(2,1)} %copy-done.4) | copy-start | bytes 1572868
  88.6 4.9 %collective-permute-start.12 = (bf16[1152,128]{1,0:T(8,128)(2,1)S(1)}, bf16[1152,128]{1,0:T(8,128)(2,1)S(1)}, u32[]{:S(2)}, u32[]{:S(2)}) collective-permute-start(bf16[1152,128]{1,0:T(8,128)(2,1)S(1)} %get-tuple-element.26), channel_id=1, source_target_pairs={{0,16},{16,0},{1,17},{17,1},{2,18},{18,2},{3,19},{19,3},{4,20},{20... | collective-permute-start | bytes 884744 | tf_op jit(solution)/shard_map/ppermute | solution.py:204
  127.4 22.5 %all-to-all-start.2 = ((bf16[24,48,128]{2,1,0:T(8,128)(2,1)}), bf16[24,48,128]{2,1,0:T(8,128)(2,1)S(1)}, u32[]{:S(2)}, u32[]{:S(2)}) async-start(bf16[24,48,128]{2,1,0:T(8,128)(2,1)} %shard_map.126), calls=%async_computation.2 | async-start | bytes 589824 | tf_op jit(solution)/shard_map/all_to_all | solution.py:239
  133.3 19.6 %collective-permute-start = (bf16[512,512]{1,0:T(8,128)(2,1)}, bf16[512,512]{1,0:T(8,128)(2,1)S(1)}, u32[]{:S(2)}, u32[]{:S(2)}) collective-permute-start(bf16[512,512]{1,0:T(8,128)(2,1)} %get-tuple-element.18), channel_id=1, source_target_pairs={{0,1},{1,2},{2,3},{3,0},{4,5},{5,6},{6,7},{7,4},{8,9},{9,10},{10,1... | collective-permute-start | bytes 1572872 | tf_op jit(solution)/shard_map/ppermute | solution.py:204
  137.1 24.0 %collective-permute-start.1 = (bf16[512,512]{1,0:T(8,128)(2,1)}, bf16[512,512]{1,0:T(8,128)(2,1)S(1)}, u32[]{:S(2)}, u32[]{:S(2)}) collective-permute-start(bf16[512,512]{1,0:T(8,128)(2,1)} %copy-done.6), channel_id=1, source_target_pairs={{0,2},{1,3},{2,0},{3,1},{4,6},{5,7},{6,4},{7,5},{8,10},{9,11},{10,... | collective-permute-start | bytes 1572872 | tf_op jit(solution)/shard_map/ppermute | solution.py:204
  140.7 22.5 %collective-permute-start.2 = (bf16[512,512]{1,0:T(8,128)(2,1)S(1)}, bf16[512,512]{1,0:T(8,128)(2,1)S(1)}, u32[]{:S(2)}, u32[]{:S(2)}) collective-permute-start(bf16[512,512]{1,0:T(8,128)(2,1)S(1)} %copy-done.5), channel_id=1, source_target_pairs={{0,3},{1,0},{2,1},{3,2},{4,7},{5,4},{6,5},{7,6},{8,11},{9,8},{10,9... | collective-permute-start | bytes 1572872 | tf_op jit(solution)/shard_map/ppermute | solution.py:204
  149.8 24.5 %copy-start.10 = (bf16[512]{0:T(512)(128)(2,1)S(1)}, bf16[512]{0:T(512)(128)(2,1)}, u32[]{:S(2)}) copy-start(bf16[512]{0:T(512)(128)(2,1)} %param.16) | copy-start | bytes 3076
  149.8 30.9 %collective-permute-start.13 = (bf16[1152,128]{1,0:T(8,128)(2,1)S(1)}, bf16[1152,128]{1,0:T(8,128)(2,1)S(1)}, u32[]{:S(2)}, u32[]{:S(2)}) collective-permute-start(bf16[1152,128]{1,0:T(8,128)(2,1)S(1)} %bitcast.4), channel_id=1, source_target_pairs={{0,16},{16,0},{1,17},{17,1},{2,18},{18,2},{3,19},{19,3},{4,20},{20... | collective-permute-start | bytes 884744 | tf_op jit(solution)/shard_map/ppermute | solution.py:204
  165.3 9.0 %collective-permute-start.3 = (bf16[128,512]{1,0:T(8,128)(2,1)S(1)}, bf16[128,512]{1,0:T(8,128)(2,1)S(1)}, u32[]{:S(2)}, u32[]{:S(2)}) collective-permute-start(bf16[128,512]{1,0:T(8,128)(2,1)S(1)} %get-tuple-element.22), channel_id=1, source_target_pairs={{0,4},{4,8},{8,12},{12,0},{1,5},{5,9},{9,13},{13,1},{2,6},{6,10},{... | collective-permute-start | bytes 393224 | tf_op jit(solution)/shard_map/ppermute | solution.py:204
  167.2 12.3 %collective-permute-start.4 = (bf16[128,512]{1,0:T(8,128)(2,1)S(1)}, bf16[128,512]{1,0:T(8,128)(2,1)S(1)}, u32[]{:S(2)}, u32[]{:S(2)}) collective-permute-start(bf16[128,512]{1,0:T(8,128)(2,1)S(1)} %get-tuple-element.23), channel_id=1, source_target_pairs={{0,8},{4,12},{8,0},{12,4},{1,9},{5,13},{9,1},{13,5},{2,10},{6,14},... | collective-permute-start | bytes 393224 | tf_op jit(solution)/shard_map/ppermute | solution.py:204
  169.1 10.4 %collective-permute-start.5 = (bf16[128,512]{1,0:T(8,128)(2,1)S(1)}, bf16[128,512]{1,0:T(8,128)(2,1)S(1)}, u32[]{:S(2)}, u32[]{:S(2)}) collective-permute-start(bf16[128,512]{1,0:T(8,128)(2,1)S(1)} %get-tuple-element.24), channel_id=1, source_target_pairs={{0,12},{4,0},{8,4},{12,8},{1,13},{5,1},{9,5},{13,9},{2,14},{6,2},{... | collective-permute-start | bytes 393224 | tf_op jit(solution)/shard_map/ppermute | solution.py:204

commit v4 on v3

--- a/solution.py
+++ b/solution.py
@@ -23,16 +23,16 @@
 MIB = 1024 * 1024
 
 
-def call(kernel, outs, args, smem=0, scratch=(), flops=0, nbytes=0, mib=50):
+def call(kernel, outs, args, smem=0, scratch=(), flops=0, nbytes=0, mib=50, raw=(), raw_outs=()):
     in_specs = [pl.BlockSpec(memory_space=pltpu.SMEM)] * smem
-    in_specs += [pl.BlockSpec(memory_space=pltpu.VMEM)] * (len(args) - smem)
+    vmem, anywhere = pl.BlockSpec(memory_space=pltpu.VMEM), pl.BlockSpec(memory_space=pl.ANY)
+    in_specs += [anywhere if i in raw else vmem for i in range(smem, len(args))]
     many = isinstance(outs, (list, tuple))
-    vmem = pl.BlockSpec(memory_space=pltpu.VMEM)
     return pl.pallas_call(
         kernel,
         out_shape=outs,
         in_specs=in_specs,
-        out_specs=[vmem] * len(outs) if many else vmem,
+        out_specs=[anywhere if i in raw_outs else vmem for i in range(len(outs))] if many else vmem,
         scratch_shapes=list(scratch),
         cost_estimate=pl.CostEstimate(flops=flops, bytes_accessed=nbytes, transcendentals=0),
         compiler_params=pltpu.CompilerParams(vmem_limit_bytes=mib * MIB),
@@ -53,18 +53,29 @@
     out_ref[...] = (cot_ref[...].astype(F32) * own_valid(length_ref, 128, 512)).astype(BF)
 
 
-def prep_kernel(text_ref, image_ref, out_ref):
-    rows = image_ref.shape[0]
-    total = jnp.zeros((rows, 512), F32)
+def prep_kernel(text_hbm, image_hbm, out_ref, text_ref, image_ref, semaphores):
+    fetched = pltpu.make_async_copy(image_hbm, image_ref, semaphores.at[4])
+    fetched.start()
+    texts = []
+    for j in range(4):
+        rows = pl.ds(j * 512, 512)
+        texts.append(pltpu.make_async_copy(text_hbm.at[rows, :], text_ref.at[rows, :], semaphores.at[j]))
+        texts[j].start()
+    fetched.wait()
+    total = jnp.zeros((64, 512), F32)
     for t in range(16):
         part = image_ref[:, t * 512 : (t + 1) * 512].astype(F32)
         total = total + part * part
     rstd = lax.rsqrt(jnp.sum(total, axis=1, keepdims=True) / D + EPS)
+    for t in range(16):
+        part = image_ref[:, t * 512 : (t + 1) * 512].astype(F32)
+        out_ref[t, :64, :] = (part * rstd).astype(BF)
     row = lax.broadcasted_iota(jnp.int32, (8, 512), 0)
     ones = jnp.ones((8, 128), F32)
     parts = jnp.zeros((8, 512), F32)
     for j in range(4):
         lanes = jnp.zeros((512, 128), F32)
+        texts[j].wait()
         for b in range(4):
             part = text_ref[j * 512 : (j + 1) * 512, b * 128 : (b + 1) * 128].astype(F32)
             lanes = lanes + part * part
@@ -76,8 +87,6 @@
         parts = parts + jnp.where(row == j, top, 0.0) + jnp.where(row == j + 4, sums - top, 0.0)
     parts = parts.astype(BF)
     for t in range(16):
-        part = image_ref[:, t * 512 : (t + 1) * 512].astype(F32)
-        out_ref[t, :64, :] = (part * rstd).astype(BF)
         out_ref[t, 64:, :] = parts
 
 
@@ -86,8 +95,18 @@
 
 
 def norm_kernel(
-    offset_ref, count_ref, text_ref, got_ref, weight_ref, gain_ref, normed_ref, key1_ref, key2_ref, key3_ref
+    offset_ref, count_ref, text_hbm, got_hbm, weight_ref, gain_ref, normed_hbm, key1_hbm, key2_hbm, key3_hbm,
+    text_ref, got_ref, normed_ref, keys_ref, semaphores, sent,
 ):
+    fetched = pltpu.make_async_copy(got_hbm, got_ref, semaphores.at[8])
+    fetched.start()
+    texts, puts = [], []
+    for i in range(8):
+        rows = pl.ds(i * 256, 256)
+        texts.append(pltpu.make_async_copy(text_hbm.at[rows, :], text_ref.at[rows, :], semaphores.at[i]))
+        texts[i].start()
+        puts.append(pltpu.make_async_copy(normed_ref.at[rows, :], normed_hbm.at[rows, :], sent.at[i]))
+    fetched.wait()
     squares = jnp.concatenate([got_ref[t, 64:, :] for t in range(16)], axis=0)
     pick = lax.broadcasted_iota(jnp.int32, (128, 128), 0) % 4
     gain = gain_ref[...].astype(F32)
@@ -113,25 +132,43 @@
             placed = jnp.dot(hot[0], images[:256], preferred_element_type=F32)
             placed = placed + jnp.dot(hot[1], images[256:], preferred_element_type=F32)
             rows = slice(seq * LEN + base, seq * LEN + base + 256)
+            texts[seq * 4 + part].wait()
             for b in range(4):
                 cols = slice(b * 128, (b + 1) * 128)
                 text = text_ref[rows, cols].astype(F32)
                 value = jnp.where(covered, placed[:, cols], text) * scale * gain[:, cols]
                 normed_ref[rows, cols] = value.astype(BF)
+            puts[seq * 4 + part].start()
     x = lax.axis_index("x")
-    for s, key_ref in enumerate((key1_ref, key2_ref, key3_ref)):
+    for s, key_hbm in enumerate((key1_hbm, key2_hbm, key3_hbm)):
         q = lax.rem(x + s + 1, 4)
         normed = jnp.concatenate([normed_ref[block(z, q), :] for z in range(4)], axis=0)
-        key_ref[...] = jnp.dot(normed, weight_ref[...], preferred_element_type=F32).astype(BF)
-
-
-def grad_kernel(normed_ref, own_ref, got1_ref, got2_ref, got3_ref, mine_ref, other_ref, grad_ref):
+        keys_ref[s] = jnp.dot(normed, weight_ref[...], preferred_element_type=F32).astype(BF)
+        puts.append(pltpu.make_async_copy(keys_ref.at[s], key_hbm, sent.at[8 + s]))
+        puts[8 + s].start()
+    for put in puts:
+        put.wait()
+
+
+def grad_kernel(
+    normed_hbm, own_hbm, got1_hbm, got2_hbm, got3_hbm, mine_ref, other_ref, grad_ref, normed_ref, masked_ref, semaphores
+):
     x, zl, core = lax.axis_index("x"), lax.axis_index("zl"), lax.axis_index("c")
     bias = jnp.zeros((8, 512), F32)
-    for s, source in enumerate((own_ref, got1_ref, got2_ref, got3_ref)):
+    copies = []
+    for s, source in enumerate((own_hbm, got1_hbm, got2_hbm, got3_hbm)):
         q = lax.rem(x - s + 4, 4)
-        normed = jnp.concatenate([normed_ref[block(lax.rem(zl - i + 4, 4), q), :] for i in range(4)], axis=0)
-        masked = source[...]
+        pairs = [(source, masked_ref.at[s])]
+        for i in range(4):
+            rows = block(lax.rem(zl - i + 4, 4), q)
+            pairs.append((normed_hbm.at[rows, :], normed_ref.at[s, pl.ds(i * 128, 128), :]))
+        copies.append([pltpu.make_async_copy(a, b, semaphores.at[s, i]) for i, (a, b) in enumerate(pairs)])
+        for copy in copies[s]:
+            copy.start()
+    for s in range(4):
+        for copy in copies[s]:
+            copy.wait()
+        normed, masked = normed_ref[s], masked_ref[s]
         part = lax.dot_general(normed, masked, (((0,), (0,)), ((), ())), preferred_element_type=F32)
         grad_ref[...] = part if s == 0 else grad_ref[...] + part
         bias = bias + jnp.dot(jnp.ones((8, 512), BF), masked, preferred_element_type=F32)
@@ -208,7 +245,16 @@
     gain = gain.reshape(1, 512)
     own = call(mask_kernel, shape((128, 512), BF), (lengths, cot), smem=1, flops=10**6, nbytes=3 * 10**5)
     column = [own] + [shift(own, "zl", s) for s in (1, 2, 3)]
-    split = call(prep_kernel, shape((16, 72, 512), BF), (text, image), flops=10**7, nbytes=5 * 10**6)
+    split = call(
+        prep_kernel,
+        shape((16, 72, 512), BF),
+        (text, image),
+        scratch=[pltpu.VMEM((2048, 512), BF), pltpu.VMEM((64, 8192), BF), pltpu.SemaphoreType.DMA((5,))],
+        flops=10**7,
+        nbytes=5 * 10**6,
+        mib=56,
+        raw=(0, 1),
+    )
     images = lax.all_to_all(split, TP, 0, 0, tiled=True)
     column = jnp.concatenate(column, axis=0)
     got = [shift(column, "x", s) for s in (1, 2, 3)]
@@ -217,6 +263,16 @@
         [shape((2048, 512), BF)] + [shape((512, 512), BF)] * 3,
         (offsets, counts, text, images, weight, gain),
         smem=2,
+        scratch=[
+            pltpu.VMEM((2048, 512), BF),
+            pltpu.VMEM((16, 72, 512), BF),
+            pltpu.VMEM((2048, 512), BF),
+            pltpu.VMEM((3, 512, 512), BF),
+            pltpu.SemaphoreType.DMA((9,)),
+            pltpu.SemaphoreType.DMA((11,)),
+        ],
+        raw=(2, 3),
+        raw_outs=(0, 1, 2, 3),
         flops=3 * 10**9,
         nbytes=8 * 10**6,
     )
@@ -228,7 +284,13 @@
         grad_kernel,
         [shape((HALF, 128), F32), shape((HALF, 128), BF)],
         (normed, column, *got),
-        scratch=[pltpu.VMEM((512, 512), F32)],
+        scratch=[
+            pltpu.VMEM((512, 512), F32),
+            pltpu.VMEM((4, 512, 512), BF),
+            pltpu.VMEM((4, 512, 512), BF),
+            pltpu.SemaphoreType.DMA((4, 5)),
+        ],
+        raw=(0, 1, 2, 3, 4),
         flops=10**9,
         nbytes=5 * 10**6,
     )

time: 185 us -> 184 us (level)
  no operation moved by 1% of the time
where the time goes in v4:
time: 184 us; the launch traced here: 181 us
  waiting for transfers between devices  66.3 us (36%)
  starting transfers between devices  61.3 us (33%)
  blocking collectives  32.9 us (18%)
  Pallas kernels  19.3 us (10%)
    ppermute x14, waiting for transfers between devices, shift(): return lax.ppermute(value, axis, [(i, (i + by) % n) for i in range(n)])  60.1 us
    ppermute x14, starting transfers between devices, shift(): return lax.ppermute(value, axis, [(i, (i + by) % n) for i in range(n)])  44.8 us
    all_to_all x1, blocking collectives, on_device(): pieces = lax.all_to_all(pieces, RING, 0, 0, tiled=True)  32.9 us
    pallas_call x8, Pallas kernels, call(): pl.pallas_call(kernel, out_shape=outs, in_specs=in_specs, out_specs=[anyw...  19.3 us
    all_to_all x1, starting transfers between devices, on_device(): images = lax.all_to_all(split, TP, 0, 0, tiled=True)  10.5 us
    all_to_all x1, waiting for transfers between devices, on_device(): half = lax.all_to_all(copies, RING, 0, 0, tiled=True).reshape(HALF, 128)  6.2 us
    all_to_all x1, starting transfers between devices, on_device(): half = lax.all_to_all(copies, RING, 0, 0, tiled=True).reshape(HALF, 128)  6 us
  transfers between devices with their start and end apart: 16, of which 10 were waited for; matrix products, arithmetic and copies ran while one was open for 0% of the time, Pallas kernels for 5%

profile of v4, /device:TPU:1, one launch (start us, length us, event | category | flops | bytes accessed | tf_op | source)
XLA Modules:
  0.0 181.0 jit_solution(13883753519393942399)
XLA Ops:
  0.6 4.3 %shard_map.120 = bf16[16,72,512]{2,1,0:T(8,128)(2,1)} custom-call(bf16[2048,512]{1,0:T(8,128)(2,1)} %text_hbm.3, bf16[64,8192]{1,0:T(8,128)(2,1)} %image_hbm.1), custom_call_target="tpu_custom_call" | custom-call | flops 10000000 | bytes 5000000 | tf_op jit(solution)/shard_map/pallas_call | solution.py:31
  4.9 0.0 copy-start.1
  4.9 0.0 copy-start.2
  4.9 0.0 copy-start.8
  5.0 0.0 copy-start
  5.0 0.0 copy-start.6
  5.0 0.0 copy-start.7
  5.0 10.5 %all-to-all-start = ((bf16[16,72,512]{2,1,0:T(8,128)(2,1)}), bf16[16,72,512]{2,1,0:T(8,128)(2,1)S(1)}, u32[]{:S(2)}, u32[]{:S(2)}) async-start(bf16[16,72,512]{2,1,0:T(8,128)(2,1)} %shard_map.120), calls=%async_computation | async-start | bytes 2359296 | tf_op jit(solution)/shard_map/all_to_all | solution.py:258
  15.5 0.6 shard_map.124
  16.1 5.1 %collective-permute-start.8 = (bf16[128,512]{1,0:T(8,128)(2,1)S(1)}, bf16[128,512]{1,0:T(8,128)(2,1)S(1)}, u32[]{:S(2)}, u32[]{:S(2)}) collective-permute-start(bf16[128,512]{1,0:T(8,128)(2,1)S(1)} %shard_map.124), channel_id=1, source_target_pairs={{0,12},{4,0},{8,4},{12,8},{1,13},{5,1},{9,5},{13,9},{2,14},{6,2},{... | collective-permute-start | bytes 393224 | tf_op jit(solution)/shard_map/ppermute | solution.py:241
  21.2 1.9 %collective-permute-start.7 = (bf16[128,512]{1,0:T(8,128)(2,1)S(1)}, bf16[128,512]{1,0:T(8,128)(2,1)S(1)}, u32[]{:S(2)}, u32[]{:S(2)}) collective-permute-start(bf16[128,512]{1,0:T(8,128)(2,1)S(1)} %shard_map.124), channel_id=1, source_target_pairs={{0,8},{4,12},{8,0},{12,4},{1,9},{5,13},{9,1},{13,5},{2,10},{6,14},... | collective-permute-start | bytes 393224 | tf_op jit(solution)/shard_map/ppermute | solution.py:241
  23.1 2.5 %collective-permute-start.6 = (bf16[128,512]{1,0:T(8,128)(2,1)S(1)}, bf16[128,512]{1,0:T(8,128)(2,1)S(1)}, u32[]{:S(2)}, u32[]{:S(2)}) collective-permute-start(bf16[128,512]{1,0:T(8,128)(2,1)S(1)} %shard_map.124), channel_id=1, source_target_pairs={{0,4},{4,8},{8,12},{12,0},{1,5},{5,9},{9,13},{13,1},{2,6},{6,10},{... | collective-permute-start | bytes 393224 | tf_op jit(solution)/shard_map/ppermute | solution.py:241
  25.6 8.5 %collective-permute-done.8 = bf16[128,512]{1,0:T(8,128)(2,1)S(1)} collective-permute-done((bf16[128,512]{1,0:T(8,128)(2,1)S(1)}, bf16[128,512]{1,0:T(8,128)(2,1)S(1)}, u32[]{:S(2)}, u32[]{:S(2)}) %collective-permute-start.8) | collective-permute-done | bytes 131104 | tf_op jit(solution)/shard_map/ppermute | solution.py:241
  34.1 20.8 %collective-permute-done.7 = bf16[128,512]{1,0:T(8,128)(2,1)S(1)} collective-permute-done((bf16[128,512]{1,0:T(8,128)(2,1)S(1)}, bf16[128,512]{1,0:T(8,128)(2,1)S(1)}, u32[]{:S(2)}, u32[]{:S(2)}) %collective-permute-start.7) | collective-permute-done | bytes 131104 | tf_op jit(solution)/shard_map/ppermute | solution.py:241
  54.8 0.0 collective-permute-done.6
  54.9 3.1 %collective-permute-start.9 = (bf16[512,512]{1,0:T(8,128)(2,1)S(1)}, bf16[512,512]{1,0:T(8,128)(2,1)S(1)}, u32[]{:S(2)}, u32[]{:S(2)}) collective-permute-start(bf16[512,512]{1,0:T(8,128)(2,1)S(1)} %pad_maximum_fusion.own_hbm), channel_id=1, source_target_pairs={{0,1},{1,2},{2,3},{3,0},{4,5},{5,6},{6,7},{7,4},{8,9},{9,10},{10,1... | collective-permute-start | bytes 1572872 | tf_op jit(solution)/shard_map/ppermute | solution.py:241
  58.0 3.2 %collective-permute-start.10 = (bf16[512,512]{1,0:T(8,128)(2,1)S(1)}, bf16[512,512]{1,0:T(8,128)(2,1)S(1)}, u32[]{:S(2)}, u32[]{:S(2)}) collective-permute-start(bf16[512,512]{1,0:T(8,128)(2,1)S(1)} %pad_maximum_fusion.own_hbm), channel_id=1, source_target_pairs={{0,2},{1,3},{2,0},{3,1},{4,6},{5,7},{6,4},{7,5},{8,10},{9,11},{10,... | collective-permute-start | bytes 1572872 | tf_op jit(solution)/shard_map/ppermute | solution.py:241
  61.1 3.1 %collective-permute-start.11 = (bf16[512,512]{1,0:T(8,128)(2,1)S(1)}, bf16[512,512]{1,0:T(8,128)(2,1)}, u32[]{:S(2)}, u32[]{:S(2)}) collective-permute-start(bf16[512,512]{1,0:T(8,128)(2,1)S(1)} %pad_maximum_fusion.own_hbm), channel_id=1, source_target_pairs={{0,3},{1,0},{2,1},{3,2},{4,7},{5,4},{6,5},{7,6},{8,11},{9,8},{10,9... | collective-permute-start | bytes 1572872 | tf_op jit(solution)/shard_map/ppermute | solution.py:241
  64.3 0.0 all-to-all-done.got_hbm
  64.3 6.0 %shard_map.121 = (bf16[2048,512]{1,0:T(8,128)(2,1)}, bf16[512,512]{1,0:T(8,128)(2,1)}, bf16[512,512]{1,0:T(8,128)(2,1)S(1)}, bf16[512,512]{1,0:T(8,128)(2,1)S(1)}) custom-call(s32[2,2]{1,0:T(2,128)S(1)} %copy-done.6, s32[2]{0:T(128)S(1)} %copy-done.7, bf16[2048,512]{1,0:T(8,128)(2,1)} %text_hbm.3, bf16[16,72,512]{2,1,0:T(8,128)(2,1)S(1)} %all-to-all-done.got_hbm, ...), custom_call_target="tpu_custom_call" | custom-call | flops 3000000000 | bytes 8000000 | tf_op jit(solution)/shard_map/pallas_call | solution.py:31
  70.3 1.1 collective-permute-done.9.got1_hbm
  71.4 8.7 %collective-permute-done.10.got2_hbm = bf16[512,512]{1,0:T(8,128)(2,1)S(1)} collective-permute-done((bf16[512,512]{1,0:T(8,128)(2,1)S(1)}, bf16[512,512]{1,0:T(8,128)(2,1)S(1)}, u32[]{:S(2)}, u32[]{:S(2)}) %collective-permute-start.10) | collective-permute-done | bytes 524320 | tf_op jit(solution)/shard_map/ppermute | solution.py:241
  80.0 4.5 %collective-permute-done.11.got3_hbm = bf16[512,512]{1,0:T(8,128)(2,1)} collective-permute-done((bf16[512,512]{1,0:T(8,128)(2,1)S(1)}, bf16[512,512]{1,0:T(8,128)(2,1)}, u32[]{:S(2)}, u32[]{:S(2)}) %collective-permute-start.11) | collective-permute-done | bytes 524320 | tf_op jit(solution)/shard_map/ppermute | solution.py:241
  84.5 3.1 %shard_map.125 = (f32[1152,128]{1,0:T(8,128)S(1)}, bf16[1152,128]{1,0:T(8,128)(2,1)S(1)}) custom-call(bf16[2048,512]{1,0:T(8,128)(2,1)} %get-tuple-element.17.normed_ref.normed_hbm, bf16[512,512]{1,0:T(8,128)(2,1)S(1)} %pad_maximum_fusion.own_hbm, bf16[512,512]{1,0:T(8,128)(2,1)S(1)} %collective-permute-done.9.got1_hbm, ...), custom_call_target="tpu_custom_call" | custom-call | flops 1000000000 | bytes 5000000 | tf_op jit(solution)/shard_map/pallas_call | solution.py:31
  87.6 3.7 %collective-permute-start.12 = (bf16[1152,128]{1,0:T(8,128)(2,1)S(1)}, bf16[1152,128]{1,0:T(8,128)(2,1)S(1)}, u32[]{:S(2)}, u32[]{:S(2)}) collective-permute-start(bf16[1152,128]{1,0:T(8,128)(2,1)S(1)} %get-tuple-element.26), channel_id=1, source_target_pairs={{0,16},{16,0},{1,17},{17,1},{2,18},{18,2},{3,19},{19,3},{4,20},{20... | collective-permute-start | bytes 884744 | tf_op jit(solution)/shard_map/ppermute | solution.py:241
  91.3 1.2 collective-permute-done.12
  92.5 0.1 add_convert_fusion
  92.6 32.9 %all_to_all.15.got_ref = bf16[24,48,128]{2,1,0:T(8,128)(2,1)S(1)} all-to-all(bf16[24,48,128]{2,1,0:T(8,128)(2,1)S(1)} %bitcast.6), channel_id=1, replica_groups=mesh['zh'=3,'y'=8,'c'=2,'zl'=4,'x'=4] {'zh','y'}, dimensions={0} | all-to-all | bytes 589824 | tf_op jit(solution)/shard_map/all_to_all | solution.py:299
  125.5 0.8 shard_map.126
  126.3 6.0 %all-to-all-start.2 = ((bf16[24,48,128]{2,1,0:T(8,128)(2,1)}), bf16[24,48,128]{2,1,0:T(8,128)(2,1)S(1)}, u32[]{:S(2)}, u32[]{:S(2)}) async-start(bf16[24,48,128]{2,1,0:T(8,128)(2,1)} %shard_map.126), calls=%async_computation.2 | async-start | bytes 589824 | tf_op jit(solution)/shard_map/all_to_all | solution.py:301
  132.3 3.8 %collective-permute-start = (bf16[512,512]{1,0:T(8,128)(2,1)}, bf16[512,512]{1,0:T(8,128)(2,1)S(1)}, u32[]{:S(2)}, u32[]{:S(2)}) collective-permute-start(bf16[512,512]{1,0:T(8,128)(2,1)} %get-tuple-element.18), channel_id=1, source_target_pairs={{0,1},{1,2},{2,3},{3,0},{4,5},{5,6},{6,7},{7,4},{8,9},{9,10},{10,1... | collective-permute-start | bytes 1572872 | tf_op jit(solution)/shard_map/ppermute | solution.py:241
  136.1 3.5 %collective-permute-start.1 = (bf16[512,512]{1,0:T(8,128)(2,1)}, bf16[512,512]{1,0:T(8,128)(2,1)S(1)}, u32[]{:S(2)}, u32[]{:S(2)}) collective-permute-start(bf16[512,512]{1,0:T(8,128)(2,1)} %copy-done.5), channel_id=1, source_target_pairs={{0,2},{1,3},{2,0},{3,1},{4,6},{5,7},{6,4},{7,5},{8,10},{9,11},{10,... | collective-permute-start | bytes 1572872 | tf_op jit(solution)/shard_map/ppermute | solution.py:241
  139.6 3.0 %collective-permute-start.2 = (bf16[512,512]{1,0:T(8,128)(2,1)S(1)}, bf16[512,512]{1,0:T(8,128)(2,1)S(1)}, u32[]{:S(2)}, u32[]{:S(2)}) collective-permute-start(bf16[512,512]{1,0:T(8,128)(2,1)S(1)} %copy-done.4), channel_id=1, source_target_pairs={{0,3},{1,0},{2,1},{3,2},{4,7},{5,4},{6,5},{7,6},{8,11},{9,8},{10,9... | collective-permute-start | bytes 1572872 | tf_op jit(solution)/shard_map/ppermute | solution.py:241
  142.6 6.2 %all-to-all-done.2 = bf16[24,48,128]{2,1,0:T(8,128)(2,1)S(1)} async-done(((bf16[24,48,128]{2,1,0:T(8,128)(2,1)}), bf16[24,48,128]{2,1,0:T(8,128)(2,1)S(1)}, u32[]{:S(2)}, u32[]{:S(2)}) %all-to-all-start.2) | async-done | bytes 294944 | tf_op jit(solution)/shard_map/all_to_all | solution.py:301
  148.8 3.0 %collective-permute-start.13 = (bf16[1152,128]{1,0:T(8,128)(2,1)S(1)}, bf16[1152,128]{1,0:T(8,128)(2,1)S(1)}, u32[]{:S(2)}, u32[]{:S(2)}) collective-permute-start(bf16[1152,128]{1,0:T(8,128)(2,1)S(1)} %bitcast.4), channel_id=1, source_target_pairs={{0,16},{16,0},{1,17},{17,1},{2,18},{18,2},{3,19},{19,3},{4,20},{20... | collective-permute-start | bytes 884744 | tf_op jit(solution)/shard_map/ppermute | solution.py:241
  151.8 0.0 collective-permute-done.a_ref
  151.8 8.2 %collective-permute-done.1.b_ref = bf16[512,512]{1,0:T(8,128)(2,1)S(1)} collective-permute-done((bf16[512,512]{1,0:T(8,128)(2,1)}, bf16[512,512]{1,0:T(8,128)(2,1)S(1)}, u32[]{:S(2)}, u32[]{:S(2)}) %collective-permute-start.1) | collective-permute-done | bytes 524320 | tf_op jit(solution)/shard_map/ppermute | solution.py:241
  160.1 2.1 %collective-permute-done.2.c_ref = bf16[512,512]{1,0:T(8,128)(2,1)S(1)} collective-permute-done((bf16[512,512]{1,0:T(8,128)(2,1)S(1)}, bf16[512,512]{1,0:T(8,128)(2,1)S(1)}, u32[]{:S(2)}, u32[]{:S(2)}) %collective-permute-start.2) | collective-permute-done | bytes 524320 | tf_op jit(solution)/shard_map/ppermute | solution.py:241
  162.1 2.1 %shard_map.122 = (f32[128,512]{1,0:T(8,128)S(1)}, bf16[128,512]{1,0:T(8,128)(2,1)S(1)}, bf16[128,512]{1,0:T(8,128)(2,1)S(1)}, bf16[128,512]{1,0:T(8,128)(2,1)S(1)}) custom-call(bf16[2048,512]{1,0:T(8,128)(2,1)} %get-tuple-element.17.normed_ref.normed_hbm, bf16[512,512]{1,0:T(8,128)(2,1)S(1)} %copy-done, bf16[512,512]{1,0:T(8,128)(2,1)S(1)} %collective-permute-done.a_ref, ...), custom_call_target="tpu_custom_call" | custom-call | flops 1000000 | bytes 4000000 | tf_op jit(solution)/shard_map/pallas_call | solution.py:31
  164.2 1.9 %collective-permute-start.3 = (bf16[128,512]{1,0:T(8,128)(2,1)S(1)}, bf16[128,512]{1,0:T(8,128)(2,1)S(1)}, u32[]{:S(2)}, u32[]{:S(2)}) collective-permute-start(bf16[128,512]{1,0:T(8,128)(2,1)S(1)} %get-tuple-element.22), channel_id=1, source_target_pairs={{0,4},{4,8},{8,12},{12,0},{1,5},{5,9},{9,13},{13,1},{2,6},{6,10},{... | collective-permute-start | bytes 393224 | tf_op jit(solution)/shard_map/ppermute | solution.py:241
  166.2 1.9 %collective-permute-start.4 = (bf16[128,512]{1,0:T(8,128)(2,1)S(1)}, bf16[128,512]{1,0:T(8,128)(2,1)S(1)}, u32[]{:S(2)}, u32[]{:S(2)}) collective-permute-start(bf16[128,512]{1,0:T(8,128)(2,1)S(1)} %get-tuple-element.23), channel_id=1, source_target_pairs={{0,8},{4,12},{8,0},{12,4},{1,9},{5,13},{9,1},{13,5},{2,10},{6,14},... | collective-permute-start | bytes 393224 | tf_op jit(solution)/shard_map/ppermute | solution.py:241
  168.1 5.2 %collective-permute-start.5 = (bf16[128,512]{1,0:T(8,128)(2,1)S(1)}, bf16[128,512]{1,0:T(8,128)(2,1)S(1)}, u32[]{:S(2)}, u32[]{:S(2)}) collective-permute-start(bf16[128,512]{1,0:T(8,128)(2,1)S(1)} %get-tuple-element.24), channel_id=1, source_target_pairs={{0,12},{4,0},{8,4},{12,8},{1,13},{5,1},{9,5},{13,9},{2,14},{6,2},{... | collective-permute-start | bytes 393224 | tf_op jit(solution)/shard_map/ppermute | solution.py:241
  173.3 0.0 collective-permute-done.3.a_ref
  173.3 5.1 %collective-permute-done.4.b_ref = bf16[128,512]{1,0:T(8,128)(2,1)S(1)} collective-permute-done((bf16[128,512]{1,0:T(8,128)(2,1)S(1)}, bf16[128,512]{1,0:T(8,128)(2,1)S(1)}, u32[]{:S(2)}, u32[]{:S(2)}) %collective-permute-start.4) | collective-permute-done | bytes 131104 | tf_op jit(solution)/shard_map/ppermute | solution.py:241
  178.4 0.0 collective-permute-done.5.c_ref
  178.5 1.3 shard_map.123
  179.7 0.0 collective-permute-done.13.other_ref
  179.7 1.2 shard_map.127
  (17 shorter events, 0.1 us)
Async XLA Ops:
  4.9 10.6 %copy-start.1 = (bf16[128,512]{1,0:T(8,128)(2,1)S(1)}, bf16[128,512]{1,0:T(8,128)(2,1)}, u32[]{:S(2)}) copy-start(bf16[128,512]{1,0:T(8,128)(2,1)} %cot_ref.1) | copy-start | bytes 393220
  4.9 10.6 %copy-start.2 = (s32[2]{0:T(128)S(1)}, s32[2]{0:T(128)}, u32[]{:S(2)}) copy-start(s32[2]{0:T(128)} %length_ref.3) | copy-start | bytes 28
  4.9 59.3 %copy-start.8 = (bf16[512]{0:T(512)(128)(2,1)S(1)}, bf16[512]{0:T(512)(128)(2,1)}, u32[]{:S(2)}) copy-start(bf16[512]{0:T(512)(128)(2,1)} %param.14) | copy-start | bytes 3076
  5.0 59.3 %copy-start = (bf16[512,512]{1,0:T(8,128)(2,1)S(1)}, bf16[512,512]{1,0:T(8,128)(2,1)}, u32[]{:S(2)}) copy-start(bf16[512,512]{1,0:T(8,128)(2,1)} %weight_ref.5) | copy-start | bytes 1572868
  5.0 59.3 %copy-start.6 = (s32[2,2]{1,0:T(2,128)S(1)}, s32[2,2]{1,0:T(2,128)}, u32[]{:S(2)}) copy-start(s32[2,2]{1,0:T(2,128)} %offset_ref.1) | copy-start | bytes 52
  5.0 59.3 %copy-start.7 = (s32[2]{0:T(128)S(1)}, s32[2]{0:T(128)}, u32[]{:S(2)}) copy-start(s32[2]{0:T(128)} %count_ref.1) | copy-start | bytes 28
  5.0 59.3 %all-to-all-start = ((bf16[16,72,512]{2,1,0:T(8,128)(2,1)}), bf16[16,72,512]{2,1,0:T(8,128)(2,1)S(1)}, u32[]{:S(2)}, u32[]{:S(2)}) async-start(bf16[16,72,512]{2,1,0:T(8,128)(2,1)} %shard_map.120), calls=%async_computation | async-start | bytes 2359296 | tf_op jit(solution)/shard_map/all_to_all | solution.py:258
  16.1 17.9 %collective-permute-start.8 = (bf16[128,512]{1,0:T(8,128)(2,1)S(1)}, bf16[128,512]{1,0:T(8,128)(2,1)S(1)}, u32[]{:S(2)}, u32[]{:S(2)}) collective-permute-start(bf16[128,512]{1,0:T(8,128)(2,1)S(1)} %shard_map.124), channel_id=1, source_target_pairs={{0,12},{4,0},{8,4},{12,8},{1,13},{5,1},{9,5},{13,9},{2,14},{6,2},{... | collective-permute-start | bytes 393224 | tf_op jit(solution)/shard_map/ppermute | solution.py:241
  21.2 33.6 %collective-permute-start.7 = (bf16[128,512]{1,0:T(8,128)(2,1)S(1)}, bf16[128,512]{1,0:T(8,128)(2,1)S(1)}, u32[]{:S(2)}, u32[]{:S(2)}) collective-permute-start(bf16[128,512]{1,0:T(8,128)(2,1)S(1)} %shard_map.124), channel_id=1, source_target_pairs={{0,8},{4,12},{8,0},{12,4},{1,9},{5,13},{9,1},{13,5},{2,10},{6,14},... | collective-permute-start | bytes 393224 | tf_op jit(solution)/shard_map/ppermute | solution.py:241
  23.1 31.7 %collective-permute-start.6 = (bf16[128,512]{1,0:T(8,128)(2,1)S(1)}, bf16[128,512]{1,0:T(8,128)(2,1)S(1)}, u32[]{:S(2)}, u32[]{:S(2)}) collective-permute-start(bf16[128,512]{1,0:T(8,128)(2,1)S(1)} %shard_map.124), channel_id=1, source_target_pairs={{0,4},{4,8},{8,12},{12,0},{1,5},{5,9},{9,13},{13,1},{2,6},{6,10},{... | collective-permute-start | bytes 393224 | tf_op jit(solution)/shard_map/ppermute | solution.py:241
  54.9 16.5 %collective-permute-start.9 = (bf16[512,512]{1,0:T(8,128)(2,1)S(1)}, bf16[512,512]{1,0:T(8,128)(2,1)S(1)}, u32[]{:S(2)}, u32[]{:S(2)}) collective-permute-start(bf16[512,512]{1,0:T(8,128)(2,1)S(1)} %pad_maximum_fusion.own_hbm), channel_id=1, source_target_pairs={{0,1},{1,2},{2,3},{3,0},{4,5},{5,6},{6,7},{7,4},{8,9},{9,10},{10,1... | collective-permute-start | bytes 1572872 | tf_op jit(solution)/shard_map/ppermute | solution.py:241
  58.0 22.1 %collective-permute-start.10 = (bf16[512,512]{1,0:T(8,128)(2,1)S(1)}, bf16[512,512]{1,0:T(8,128)(2,1)S(1)}, u32[]{:S(2)}, u32[]{:S(2)}) collective-permute-start(bf16[512,512]{1,0:T(8,128)(2,1)S(1)} %pad_maximum_fusion.own_hbm), channel_id=1, source_target_pairs={{0,2},{1,3},{2,0},{3,1},{4,6},{5,7},{6,4},{7,5},{8,10},{9,11},{10,... | collective-permute-start | bytes 1572872 | tf_op jit(solution)/shard_map/ppermute | solution.py:241
  61.1 23.4 %collective-permute-start.11 = (bf16[512,512]{1,0:T(8,128)(2,1)S(1)}, bf16[512,512]{1,0:T(8,128)(2,1)}, u32[]{:S(2)}, u32[]{:S(2)}) collective-permute-start(bf16[512,512]{1,0:T(8,128)(2,1)S(1)} %pad_maximum_fusion.own_hbm), channel_id=1, source_target_pairs={{0,3},{1,0},{2,1},{3,2},{4,7},{5,4},{6,5},{7,6},{8,11},{9,8},{10,9... | collective-permute-start | bytes 1572872 | tf_op jit(solution)/shard_map/ppermute | solution.py:241
  70.3 17.3 %copy-start.3 = (bf16[512,512]{1,0:T(8,128)(2,1)}, bf16[512,512]{1,0:T(8,128)(2,1)S(1)}, u32[]{:S(2)}) copy-start(bf16[512,512]{1,0:T(8,128)(2,1)S(1)} %get-tuple-element.20) | copy-start | bytes 1572868
  70.3 22.3 %copy-start.5 = (bf16[512,512]{1,0:T(8,128)(2,1)}, bf16[512,512]{1,0:T(8,128)(2,1)S(1)}, u32[]{:S(2)}) copy-start(bf16[512,512]{1,0:T(8,128)(2,1)S(1)} %get-tuple-element.19) | copy-start | bytes 1572868
  87.6 52.0 %copy-start.4 = (bf16[512,512]{1,0:T(8,128)(2,1)S(1)}, bf16[512,512]{1,0:T(8,128)(2,1)}, u32[]{:S(2)}) copy-start(bf16[512,512]{1,0:T(8,128)(2,1)} %copy-done.3) | copy-start | bytes 1572868
  87.6 4.9 %collective-permute-start.12 = (bf16[1152,128]{1,0:T(8,128)(2,1)S(1)}, bf16[1152,128]{1,0:T(8,128)(2,1)S(1)}, u32[]{:S(2)}, u32[]{:S(2)}) collective-permute-start(bf16[1152,128]{1,0:T(8,128)(2,1)S(1)} %get-tuple-element.26), channel_id=1, source_target_pairs={{0,16},{16,0},{1,17},{17,1},{2,18},{18,2},{3,19},{19,3},{4,20},{20... | collective-permute-start | bytes 884744 | tf_op jit(solution)/shard_map/ppermute | solution.py:241
  126.3 22.6 %all-to-all-start.2 = ((bf16[24,48,128]{2,1,0:T(8,128)(2,1)}), bf16[24,48,128]{2,1,0:T(8,128)(2,1)S(1)}, u32[]{:S(2)}, u32[]{:S(2)}) async-start(bf16[24,48,128]{2,1,0:T(8,128)(2,1)} %shard_map.126), calls=%async_computation.2 | async-start | bytes 589824 | tf_op jit(solution)/shard_map/all_to_all | solution.py:301
  132.3 19.6 %collective-permute-start = (bf16[512,512]{1,0:T(8,128)(2,1)}, bf16[512,512]{1,0:T(8,128)(2,1)S(1)}, u32[]{:S(2)}, u32[]{:S(2)}) collective-permute-start(bf16[512,512]{1,0:T(8,128)(2,1)} %get-tuple-element.18), channel_id=1, source_target_pairs={{0,1},{1,2},{2,3},{3,0},{4,5},{5,6},{6,7},{7,4},{8,9},{9,10},{10,1... | collective-permute-start | bytes 1572872 | tf_op jit(solution)/shard_map/ppermute | solution.py:241
  136.1 24.0 %collective-permute-start.1 = (bf16[512,512]{1,0:T(8,128)(2,1)}, bf16[512,512]{1,0:T(8,128)(2,1)S(1)}, u32[]{:S(2)}, u32[]{:S(2)}) collective-permute-start(bf16[512,512]{1,0:T(8,128)(2,1)} %copy-done.5), channel_id=1, source_target_pairs={{0,2},{1,3},{2,0},{3,1},{4,6},{5,7},{6,4},{7,5},{8,10},{9,11},{10,... | collective-permute-start | bytes 1572872 | tf_op jit(solution)/shard_map/ppermute | solution.py:241
  139.6 22.5 %collective-permute-start.2 = (bf16[512,512]{1,0:T(8,128)(2,1)S(1)}, bf16[512,512]{1,0:T(8,128)(2,1)S(1)}, u32[]{:S(2)}, u32[]{:S(2)}) collective-permute-start(bf16[512,512]{1,0:T(8,128)(2,1)S(1)} %copy-done.4), channel_id=1, source_target_pairs={{0,3},{1,0},{2,1},{3,2},{4,7},{5,4},{6,5},{7,6},{8,11},{9,8},{10,9... | collective-permute-start | bytes 1572872 | tf_op jit(solution)/shard_map/ppermute | solution.py:241
  148.8 24.4 %copy-start.9 = (bf16[512]{0:T(512)(128)(2,1)S(1)}, bf16[512]{0:T(512)(128)(2,1)}, u32[]{:S(2)}) copy-start(bf16[512]{0:T(512)(128)(2,1)} %param.16) | copy-start | bytes 3076
  148.8 30.9 %collective-permute-start.13 = (bf16[1152,128]{1,0:T(8,128)(2,1)S(1)}, bf16[1152,128]{1,0:T(8,128)(2,1)S(1)}, u32[]{:S(2)}, u32[]{:S(2)}) collective-permute-start(bf16[1152,128]{1,0:T(8,128)(2,1)S(1)} %bitcast.4), channel_id=1, source_target_pairs={{0,16},{16,0},{1,17},{17,1},{2,18},{18,2},{3,19},{19,3},{4,20},{20... | collective-permute-start | bytes 884744 | tf_op jit(solution)/shard_map/ppermute | solution.py:241
  164.2 9.0 %collective-permute-start.3 = (bf16[128,512]{1,0:T(8,128)(2,1)S(1)}, bf16[128,512]{1,0:T(8,128)(2,1)S(1)}, u32[]{:S(2)}, u32[]{:S(2)}) collective-permute-start(bf16[128,512]{1,0:T(8,128)(2,1)S(1)} %get-tuple-element.22), channel_id=1, source_target_pairs={{0,4},{4,8},{8,12},{12,0},{1,5},{5,9},{9,13},{13,1},{2,6},{6,10},{... | collective-permute-start | bytes 393224 | tf_op jit(solution)/shard_map/ppermute | solution.py:241
  166.2 12.3 %collective-permute-start.4 = (bf16[128,512]{1,0:T(8,128)(2,1)S(1)}, bf16[128,512]{1,0:T(8,128)(2,1)S(1)}, u32[]{:S(2)}, u32[]{:S(2)}) collective-permute-start(bf16[128,512]{1,0:T(8,128)(2,1)S(1)} %get-tuple-element.23), channel_id=1, source_target_pairs={{0,8},{4,12},{8,0},{12,4},{1,9},{5,13},{9,1},{13,5},{2,10},{6,14},... | collective-permute-start | bytes 393224 | tf_op jit(solution)/shard_map/ppermute | solution.py:241
  168.1 10.4 %collective-permute-start.5 = (bf16[128,512]{1,0:T(8,128)(2,1)S(1)}, bf16[128,512]{1,0:T(8,128)(2,1)S(1)}, u32[]{:S(2)}, u32[]{:S(2)}) collective-permute-start(bf16[128,512]{1,0:T(8,128)(2,1)S(1)} %get-tuple-element.24), channel_id=1, source_target_pairs={{0,12},{4,0},{8,4},{12,8},{1,13},{5,1},{9,5},{13,9},{2,14},{6,2},{... | collective-permute-start | bytes 393224 | tf_op jit(solution)/shard_map/ppermute | solution.py:241
